TPU v7x, 512 devices: a 8x2x16 block of a 8x8x16 slice. The times are simulated.
512 devices in a mesh: member: 2 (over y), blk: 256 (over z, x, core).
Axes of the slice: x: 8, y: 2, z: 16, core: 2. Of those that a mesh axis runs over, the one named last changes fastest.
The devices are a block of a 8x8x16 slice.
Arguments:
- pressure: float32 [55, 131072], P(None, ('member', 'blk')), parts along dimension 1, may hold values from -6 to 6
- velocity: float32 [55, 393216], P(None, ('member', 'blk')), parts along dimension 1, may hold values from -3 to 3
- tracers: float32 [3, 55, 131072], P(None, None, ('member', 'blk')), parts along dimension 2, may hold values from 0.1 to 2
- tendency: float32 [55, 131072], P(None, ('member', 'blk')), parts along dimension 1, may hold values from -6 to 6
- pattern: float32 [131072], P(('member', 'blk')), parts along dimension 0, may hold values from -0.9 to 0.9
- coupling: float32 [55, 65536], P(None, 'blk'), may hold values from 0.3 to 3
- edge_length: float32 [196608], P('blk'), may hold values from 0.7 to 1.4
- inv_distance: float32 [196608], P('blk'), may hold values from 0.7 to 1.4
- inv_area: float32 [65536], P('blk'), may hold values from 0.7 to 1.4
- edge_ends: int32 [2, 196608], P(None, 'blk'), may hold values from 0 to 351, as said below
- halo_ends: int32 [2, 32768], P(None, 'blk'), may hold values from 0 to 351, as said below
- cell_edges: int32 [8, 65536], P(None, 'blk'), may hold values from 0 to 895, as said below
- cell_signs: int32 [8, 65536], P(None, 'blk'), may hold values from -1 to 1, as said below
- cell_send: int32 [6, 4096], P(None, 'blk'), may hold values from 0 to 255, as said below
- edge_send: int32 [4, 8192], P(None, 'blk'), may hold values from 0 to 767, as said below
Outputs:
- new_pressure: float32 [55, 131072], P(None, ('member', 'blk')), parts along dimension 1
- new_velocity: float32 [55, 393216], P(None, ('member', 'blk')), parts along dimension 1
- new_tracers: float32 [3, 55, 131072], P(None, None, ('member', 'blk')), parts along dimension 2
There are 2 independent parts, one for each index of `member`. A program takes and returns all parts, laid end to end along the dimension named above; an argument that names none is the same for every part. Nothing has to cross between parts.
Inputs may be any that keep to these rules, and one draw needn't show every extreme that they name: `cell_send`: the cells form a periodic hexagonal lattice; each device holds a 16 x 16 patch, numbered in a drawn order; a patch touches the patches of the devices at index offsets 1, -1, 16, -16, 15 and 1 - 16 (modulo 256). Row k of a device's block lists the own cells that the device at index + o_k receives, o = (1, -1, 16, -16, 15, 1 - 16); rows 0 to 3 hold 16 live entries, rows 4 and 5 one live entry first, the rest repeat it. `edge_send`: row k of a device's block lists the own edges that the device at index + p_k receives, p = (1, 16, -16, 1 - 16); the live entries come first, 31, 16, 15 and 1 of them, the rest repeat a live one. `edge_ends`: row 0 is an own cell; row 1 is the neighbouring cell, own or received; the numbering is consistent with cell_send. `halo_ends`: for live received slots, the owner's edge's start and end as the receiver numbers them; other slots hold cells that no output reads. `cell_edges`: each own cell lists its six edges once each, in a drawn order, and two unused entries, whose sign is 0. `cell_signs`: 1 where the cell is the edge's start, -1 where it is its end, 0 on the unused entries.
All inputs are finite; a program needn't handle non-finite values.
Results may differ from a plain program's by a relative error of at most 0.0003.
Values sent between devices are 32-bit elements; how exact they have to be, the bound alone decides.
No kernel may reach another device: no remote copies, remote signals or barrier semaphores. Data moves between devices by JAX's collectives and lax.ppermute only.
A program may use at most 128 MiB of HBM per device.

v0:
```python
import functools

import jax
import jax.numpy as jnp
from jax import lax
from jax.experimental import pallas as pl
from jax.experimental.pallas import tpu as pltpu
from jax.sharding import PartitionSpec as P

SUBSTEPS = 6
grad_scale = 0.25
spread_scale = 0.25
force_scale = 0.5
tracer_scale = 0.05

SIDE = 16
CELLS = SIDE * SIDE
DEPTH = SUBSTEPS
COL = 32
PAD_A = 8
GROUP = 56
F32 = jnp.float32
BF16 = jnp.bfloat16
I32 = jnp.int32


def iota(shape, dim):
    return lax.broadcasted_iota(I32, shape, dim)


def one_hot(row, count):
    return jnp.where(iota((count, row.shape[1]), 0) == row, 1.0, 0.0).astype(BF16)


def halves(x):
    hi = x.astype(BF16)
    return hi, (x - hi.astype(F32)).astype(BF16)


def dot(x, y):
    return lax.dot_general(x, y, (((1,), (0,)), ((), ())), preferred_element_type=F32)


def dot_t(x, y):
    return lax.dot_general(x, y, (((1,), (1,)), ((), ())), preferred_element_type=F32)


def pick(x, table):
    hi, lo = halves(x)
    return dot(hi, table) + dot(lo, table)


def pick_t(x, table):
    hi, lo = halves(x)
    return dot_t(hi, table) + dot_t(lo, table)


def rows8(*rows):
    width = rows[0].shape[1]
    at = iota((8, width), 0)
    out = jnp.zeros((8, width), F32)
    for number, row in enumerate(rows):
        out = jnp.where(at == number, row, out)
    return out


def sixth(j):
    return (j * 43) >> 8


def prepare(
    send_ref, p_ref, vel_ref, trc_ref, tend_ref, pat_ref, coup_ref, len_ref, invd_ref, ia_ref, ends_ref,
    own_ref, trcl_ref, up_ref, dn_ref, east_ref, west_ref, meta_ref,
    x_ref, v_ref,
):
    levels = p_ref.shape[0]
    edges = vel_ref.shape[1]
    start = ends_ref[0:1, :]
    end = ends_ref[1:2, :]
    start_hot = one_hot(start, CELLS)
    end_hot = one_hot(end, CELLS)
    adjacent = dot_t(
        jnp.concatenate([start_hot, end_hot], axis=1), jnp.concatenate([end_hot, start_hot], axis=1)
    ).astype(BF16)
    cell = iota((1, CELLS), 1)
    seeds = []
    for side in (1, 0, 3, 2):
        hit = cell == send_ref[side, 0]
        for s in range(1, SIDE):
            hit = hit | (cell == send_ref[side, s])
        seeds.append(jnp.where(hit, 1.0, 0.0))
    reached = rows8(*seeds)
    far = 1.0 - reached
    for _ in range(SIDE // 2 - 1):
        reached = jnp.minimum(1.0, reached + dot(reached.astype(BF16), adjacent))
        far = far + (1.0 - reached)
    half = SIDE // 2
    a = jnp.where(far[0:1] < half, far[0:1], SIDE - 1.0 - far[1:2])
    b = jnp.where(far[2:3] < half, far[2:3], SIDE - 1.0 - far[3:4])
    place = (a * SIDE + b).astype(I32)
    corners = rows8(a, b).astype(BF16)
    at_start = dot(corners, start_hot)
    at_end = dot(corners, end_hot)
    a_s, b_s = at_start[0:1], at_start[1:2]
    a_e, b_e = at_end[0:1], at_end[1:2]
    rim_hot = one_hot(end - CELLS, 6 * SIDE)
    met = dot_t(rows8(b_s, jnp.ones_like(b_s)).astype(BF16), rim_hot)
    rim_b = jnp.where(met[1:2] > 1.5, (met[0:1] - 1.0) * 0.5, met[0:1])
    rim_b = dot(rows8(rim_b).astype(BF16), rim_hot)[0:1]
    outside = end >= CELLS
    peer = (end - CELLS) >> 4
    zero = jnp.zeros_like(end)
    direction_out = jnp.where(
        peer == 3, zero + 1, jnp.where(peer == 1, jnp.where(jnp.abs(b_s - rim_b) < 0.5, zero, zero + 2), zero + 2)
    )
    da = a_e - a_s
    db = b_e - b_s
    direction_in = jnp.where(jnp.abs(db) < 0.5, zero, jnp.where(jnp.abs(da) < 0.5, zero + 1, zero + 2))
    onward = outside | (da > 0.5) | ((jnp.abs(da) < 0.5) & (db > 0.5))
    direction = jnp.where(outside, direction_out, direction_in)
    sense = jnp.where(onward, 1.0, -1.0)
    anchor = jnp.where(onward, a_s * SIDE + b_s, a_e * SIDE + b_e).astype(I32)
    spot = direction * CELLS + anchor
    at8 = iota((8, edges), 0)
    meta = jnp.where(at8 == 0, spot, jnp.where(at8 == 1, sense.astype(I32), zero))
    meta_ref[...] = meta
    meta_ref[2:3, 0:CELLS] = place
    x_ref[...] = jnp.zeros(x_ref.shape, F32)
    height = iota((levels, 1), 0).astype(F32)
    taper = jnp.minimum(1.0, (levels - 1.0 - height) / (0.25 * levels))
    x_ref[0:levels] = p_ref[...]
    x_ref[GROUP : GROUP + levels] = force_scale * (1.0 + pat_ref[...] * taper) * tend_ref[...]
    x_ref[2 * GROUP : 2 * GROUP + levels] = coup_ref[...]
    x_ref[3 * GROUP : 3 * GROUP + 1] = ia_ref[...]
    first = 3 * GROUP + 8
    for n in range(trc_ref.shape[0]):
        x_ref[first + n * GROUP : first + n * GROUP + levels] = trc_ref[n]
    place_hot = one_hot(place, CELLS)
    moved = pick_t(x_ref[...], place_hot)
    own_ref[0 : 3 * GROUP] = moved[0 : 3 * GROUP]
    trcl_ref[...] = moved[first:]
    v_ref[...] = jnp.zeros(v_ref.shape, F32)
    v_ref[0:levels] = vel_ref[...] * sense
    v_ref[GROUP : GROUP + 1] = len_ref[...]
    v_ref[GROUP + 1 : GROUP + 2] = invd_ref[...]
    v_hi, v_lo = halves(v_ref[...])
    lengths, distances = [], []
    for k in range(3):
        spot_hot = one_hot(spot - k * CELLS, CELLS)
        got = dot_t(v_hi, spot_hot) + dot_t(v_lo, spot_hot)
        own_ref[(3 + k) * GROUP : (4 + k) * GROUP] = got[0:GROUP]
        lengths.append(got[GROUP : GROUP + 1])
        distances.append(got[GROUP + 1 : GROUP + 2])
    own_ref[6 * GROUP : 6 * GROUP + 8] = rows8(*lengths, *distances, moved[3 * GROUP : 3 * GROUP + 1])
    column = iota((1, 512), 1)
    part = column >> 7
    j = column & 127
    sa = sixth(j)
    sb = j - sa * 6
    strip = jnp.where(
        part == 0, sa * SIDE + SIDE - DEPTH + sb,
        jnp.where(part == 1, sa * SIDE + sb, jnp.where(part == 2, j + CELLS - DEPTH * SIDE, j)),
    )
    strip = jnp.where(j < DEPTH * SIDE, strip, -1)
    t = j - DEPTH * SIDE
    rim = jnp.where(
        part == 0, t * SIDE + SIDE - 1, jnp.where(part == 1, t * SIDE, jnp.where(part == 2, t + CELLS - SIDE, t))
    )
    rim = jnp.where((t >= 0) & (t < SIDE), rim, -1)
    strips = pick(own_ref[...], one_hot(strip, CELLS))
    rims = pick(trcl_ref[...], one_hot(rim, CELLS))
    top = strips[0 : rims.shape[0]] + rims
    rest = strips[rims.shape[0] :]
    for number, ref in enumerate((up_ref, dn_ref, east_ref, west_ref)):
        ref[0 : rims.shape[0]] = top[:, 128 * number : 128 * number + 128]
        ref[rims.shape[0] :] = rest[:, 128 * number : 128 * number + 128]


def advance(
    own_ref, trcl_ref, south_ref, north_ref, west_ref, east_ref, meta_ref, vel_ref, invd_ref,
    newp_ref, newv_ref, newt_ref,
    big_ref, trc_ref, hist_ref, t_ref, f_ref, inv_ref, al_ref, be_ref, out_ref, dq_ref,
):
    levels = newp_ref.shape[0]
    species = newt_ref.shape[0]
    edges = newv_ref.shape[1]
    rows = own_ref.shape[0]
    trows = trcl_ref.shape[0]
    q = iota((1, 512), 1)
    qa = q >> 5
    qb = (q & 31) - DEPTH
    inside = (qb >= 0) & (qb < SIDE)
    below = (qb >= -DEPTH) & (qb < 0)
    above = (qb >= SIDE) & (qb < SIDE + DEPTH)
    src = jnp.where(
        inside, qa * SIDE + qb,
        jnp.where(below, 256 + qa * DEPTH + qb + DEPTH, jnp.where(above, 384 + qa * DEPTH + qb - SIDE, -1)),
    )
    tsrc = jnp.where(
        inside, qa * SIDE + qb, jnp.where(qb == -1, 256 + 96 + qa, jnp.where(qb == SIDE, 384 + 96 + qa, -1))
    )
    s_val, n_val = south_ref[...], north_ref[...]
    core = pick(jnp.concatenate([own_ref[...], s_val, n_val], axis=1), one_hot(src, 512))
    tcore = pick(
        jnp.concatenate([trcl_ref[...], s_val[0:trows], n_val[0:trows]], axis=1), one_hot(tsrc, 512)
    )
    for s in range(4):
        big_ref[pl.ds(2 + s, rows, stride=8), :] = core[:, 128 * s : 128 * s + 128]
        trc_ref[pl.ds(2 + s, trows, stride=8), :] = tcore[:, 128 * s : 128 * s + 128]
    q = iota((1, 256), 1)
    qb = (q & 31) - DEPTH
    inside = (qb >= 0) & (qb < SIDE)
    below = (qb >= -DEPTH) & (qb < 0)
    above = (qb >= SIDE) & (qb < SIDE + DEPTH)
    for side, ref in ((0, west_ref), (6, east_ref)):
        qa = (q >> 5) - (PAD_A - DEPTH if side == 0 else 0)
        src = jnp.where(
            inside, qa * SIDE + qb,
            jnp.where(below, 112 + qa * DEPTH + qb + DEPTH, jnp.where(above, 148 + qa * DEPTH + qb - SIDE, -1)),
        )
        src = jnp.where((qa >= 0) & (qa < DEPTH), src, -1)
        near = DEPTH - 1 if side == 0 else 0
        tsrc = jnp.where(
            inside, 96 + qb, jnp.where(qb == -1, 184, jnp.where(qb == SIDE, 185, -1))
        )
        tsrc = jnp.where(qa == near, tsrc, -1)
        hi, lo = halves(ref[...])
        hot = one_hot(src, 256)
        thot = one_hot(tsrc, 256)
        flank = dot(hi, hot) + dot(lo, hot)
        tflank = dot(hi[0:trows], thot) + dot(lo[0:trows], thot)
        for s in range(2):
            big_ref[pl.ds(side + s, rows, stride=8), :] = flank[:, 128 * s : 128 * s + 128]
            trc_ref[pl.ds(side + s, trows, stride=8), :] = tflank[:, 128 * s : 128 * s + 128]

    lane = iota((8, 128), 1)
    first_group = lane < COL
    last_group = lane >= 128 - COL

    def b_up(x):
        return pltpu.roll(x, 127, 1)

    def b_dn(x):
        return pltpu.roll(x, 1, 1)

    def a_up(x):
        y = pltpu.roll(x, 128 - COL, 1)
        return jnp.where(last_group, pltpu.roll(y, 7, 0), y)

    def a_dn(x):
        y = pltpu.roll(x, COL, 1)
        return jnp.where(first_group, pltpu.roll(y, 1, 0), y)

    def ups(x):
        right = a_up(x)
        return right, b_up(x), b_dn(right)

    def back(x0, x1, x2):
        return a_dn(x0), b_dn(x1), b_up(a_dn(x2))

    def row(ref, number):
        return ref[8 * number : 8 * number + 8, :]

    def dyn(ref, number):
        return ref[pl.ds(pl.multiple_of(8 * number, 8), 8), :]

    length = [row(big_ref, 6 * GROUP + k) for k in range(3)]
    grad = [grad_scale * row(big_ref, 6 * GROUP + 3 + k) for k in range(3)]
    area = row(big_ref, 6 * GROUP + 6)
    pull = spread_scale * area
    out_coef = [length[k] * grad[k] for k in range(3)]
    in_coef = back(*out_coef)
    out_coef = [pull * c for c in out_coef]
    in_coef = [pull * c for c in in_coef]
    mid_coef = -(out_coef[0] + out_coef[1] + out_coef[2] + in_coef[0] + in_coef[1] + in_coef[2])

    def first_spread(l, carry):
        w = [length[k] * dyn(big_ref, (3 + k) * GROUP + l) for k in range(3)]
        w_in = back(*w)
        total = (w[0] - w_in[0]) + (w[1] - w_in[1]) + (w[2] - w_in[2])
        at = pl.ds(pl.multiple_of(8 * l, 8), 8)
        t_ref[at, :] = dyn(big_ref, GROUP + l) - pull * total
        hist_ref[at, :] = dyn(big_ref, l)
        return carry

    lax.fori_loop(0, levels, first_spread, 0, unroll=5)

    middle = levels // 2
    c = [row(big_ref, 2 * GROUP + l) for l in range(levels)] + [jnp.zeros((8, 128), F32)]
    diag = [1.0 + c[l] + c[l + 1] for l in range(levels)]
    inverse = [None] * levels
    older, old = None, jnp.ones((8, 128), F32)
    for l in range(middle):
        new = diag[l] * old if older is None else diag[l] * old - c[l] * c[l] * older
        inverse[l] = old / new
        older, old = old, new
    older, old = None, jnp.ones((8, 128), F32)
    for l in range(levels - 1, middle, -1):
        new = diag[l] * old if older is None else diag[l] * old - c[l + 1] * c[l + 1] * older
        inverse[l] = old / new
        older, old = old, new
    m = middle
    inverse[m] = 1.0 / (
        diag[m] - c[m] * c[m] * inverse[m - 1] - c[m + 1] * c[m + 1] * inverse[m + 1]
    )
    for l in range(levels):
        inv_ref[8 * l : 8 * l + 8, :] = inverse[l]
        al_ref[8 * l : 8 * l + 8, :] = c[l] * inverse[l]
        be_ref[8 * l : 8 * l + 8, :] = c[l + 1] * inverse[l]

    def substep(n, carry):
        here = n * (levels * 8)
        there = here + levels * 8

        def source(l):
            p = hist_ref[pl.ds(pl.multiple_of(here + 8 * l, 8), 8), :]
            right = a_up(p)
            left = a_dn(p)
            t = row(t_ref, l) + mid_coef * p
            t = t + (out_coef[0] * right + in_coef[0] * left)
            t = t + (out_coef[1] * b_up(p) + in_coef[1] * b_dn(p))
            t = t + (out_coef[2] * b_dn(right) + in_coef[2] * b_up(left))
            t_ref[8 * l : 8 * l + 8, :] = t
            return (p + t) * row(inv_ref, l)

        def put(l, value):
            hist_ref[pl.ds(pl.multiple_of(there + 8 * l, 8), 8), :] = value

        low = high = None
        for l in range(middle):
            h = levels - 1 - l
            low = source(l) if low is None else source(l) + row(al_ref, l) * low
            high = source(h) if high is None else source(h) + row(be_ref, h) * high
            f_ref[8 * l : 8 * l + 8, :] = low
            f_ref[8 * h : 8 * h + 8, :] = high
        low = high = source(middle) + row(al_ref, middle) * low + row(be_ref, middle) * high
        put(middle, low)
        for l in range(middle - 1, -1, -1):
            h = levels - 1 - l
            low = row(f_ref, l) + row(be_ref, l) * low
            high = row(f_ref, h) + row(al_ref, h) * high
            put(l, low)
            put(h, high)
        return carry

    lax.fori_loop(0, SUBSTEPS, substep, 0)

    scale = [g * (1.0 / SUBSTEPS) for g in grad]
    drain = tracer_scale * area

    def finish(l, carry):
        at = pl.ds(pl.multiple_of(8 * l, 8), 8)
        total = None
        weighted = None
        for n in range(SUBSTEPS):
            p = hist_ref[pl.ds(pl.multiple_of(8 * (levels * n + l), 8), 8), :]
            total = p if total is None else total + p
            weighted = total if weighted is None else weighted + total
        out_ref[at, :] = hist_ref[pl.ds(pl.multiple_of(8 * (levels * SUBSTEPS + l), 8), 8), :]
        toward, away = [], []
        shifted = ups(total)
        weight_shift = ups(weighted)
        for k in range(3):
            dq_ref[pl.ds(pl.multiple_of(8 * (GROUP * k + l), 8), 8), :] = shifted[k] - total
            mean = dyn(big_ref, (3 + k) * GROUP + l) - scale[k] * (weight_shift[k] - weighted)
            toward.append(length[k] * jnp.maximum(mean, 0.0))
            away.append(length[k] * jnp.minimum(mean, 0.0))
        for s in range(species):
            tr = dyn(trc_ref, s * GROUP + l)
            beyond = ups(tr)
            flux = [toward[k] * tr + away[k] * beyond[k] for k in range(3)]
            flux_in = back(*flux)
            spread = (flux[0] - flux_in[0]) + (flux[1] - flux_in[1]) + (flux[2] - flux_in[2])
            out_ref[pl.ds(pl.multiple_of(8 * ((s + 1) * GROUP + l), 8), 8), :] = tr - drain * spread
        return carry

    lax.fori_loop(0, levels, finish, 0, unroll=5)

    place = meta_ref[2:3, 0:CELLS]
    spot = ((place >> 4) << 5) + (place & 15) + DEPTH
    cells = jnp.concatenate([out_ref[pl.ds(2 + s, 4 * GROUP, stride=8), :] for s in range(4)], axis=1)
    cells = pick(cells, one_hot(spot, 512))
    newp_ref[...] = cells[0:levels]
    for s in range(species):
        newt_ref[s] = cells[(s + 1) * GROUP : (s + 1) * GROUP + levels]
    spot = meta_ref[0:1, :]
    turned = jnp.zeros((GROUP, edges), F32)
    for k in range(3):
        place = spot - k * CELLS
        lane_of = ((place >> 4) << 5) + (place & 15) + DEPTH
        lane_of = jnp.where((place >= 0) & (place < CELLS), lane_of, -1)
        part = jnp.concatenate(
            [dq_ref[pl.ds(8 * GROUP * k + 2 + s, GROUP, stride=8), :] for s in range(4)], axis=1
        )
        turned = turned + pick(part, one_hot(lane_of, 512))
    sense = meta_ref[1:2, :].astype(F32)
    newv_ref[...] = vel_ref[...] - (grad_scale * sense * invd_ref[...]) * turned[0:levels]


def passed_along(value, axis, steps):
    count = lax.axis_size(axis)
    pairs = [(source, (source + steps) % count) for source in range(count)]
    return lax.ppermute(value, axis, pairs)


INTERPRET = False


def per_device(
    pressure, velocity, tracers, tendency, pattern, coupling, edge_length, inv_distance, inv_area,
    edge_ends, halo_ends, cell_edges, cell_signs, cell_send, edge_send,
):
    levels, edges = velocity.shape
    species = tracers.shape[0]
    stride = lax.axis_size("blk") // 16
    rows = 6 * GROUP + 8
    trows = species * GROUP
    invd_row = inv_distance[None, :]
    shape = jax.ShapeDtypeStruct
    vmem = pl.BlockSpec(memory_space=pltpu.VMEM)
    own, trc, up, down, east, west, meta = pl.pallas_call(
        prepare,
        out_shape=(
            shape((rows, CELLS), F32), shape((trows, CELLS), F32),
            shape((rows, 128), F32), shape((rows, 128), F32), shape((rows, 128), F32), shape((rows, 128), F32),
            shape((8, edges), I32),
        ),
        in_specs=[pl.BlockSpec(memory_space=pltpu.SMEM)] + [vmem] * 10,
        out_specs=(vmem,) * 7,
        scratch_shapes=[pltpu.VMEM((3 * GROUP + 8 + trows, CELLS), F32), pltpu.VMEM((GROUP + 8, edges), F32)],
        interpret=INTERPRET,
        name="prepare",
    )(
        cell_send, pressure, velocity, tracers, tendency, pattern[None, :], coupling, edge_length[None, :],
        invd_row, inv_area[None, :], edge_ends,
    )
    south = passed_along(up, "blk", stride)
    north = passed_along(down, "blk", -stride)
    blank = jnp.zeros((rows, 70), F32)
    cut = DEPTH * DEPTH
    wide = DEPTH * SIDE
    to_east = jnp.concatenate(
        [east[:, :112], south[:, wide - cut : wide], north[:, wide - cut : wide],
         south[:, wide + 15 : wide + 16], north[:, wide + 15 : wide + 16], blank], axis=1,
    )
    to_west = jnp.concatenate(
        [west[:, :112], south[:, :cut], north[:, :cut],
         south[:, wide : wide + 1], north[:, wide : wide + 1], blank], axis=1,
    )
    from_west = passed_along(to_east, "blk", 1)
    from_east = passed_along(to_west, "blk", -1)
    block = pltpu.VMEM((levels * 8, 128), F32)
    return pl.pallas_call(
        advance,
        out_shape=(
            shape((levels, CELLS), F32), shape((levels, edges), F32), shape((species, levels, CELLS), F32),
        ),
        in_specs=[vmem] * 9,
        out_specs=(vmem,) * 3,
        scratch_shapes=[
            pltpu.VMEM((rows * 8, 128), F32), pltpu.VMEM((trows * 8, 128), F32),
            pltpu.VMEM(((SUBSTEPS + 1) * levels * 8, 128), F32),
            block, block, block, block, block,
            pltpu.VMEM((4 * GROUP * 8, 128), F32), pltpu.VMEM((3 * GROUP * 8, 128), F32),
        ],
        interpret=INTERPRET,
        name="advance",
    )(own, trc, south, north, from_west, from_east, meta, velocity, invd_row)


def solution(mesh):
    both = ("member", "blk")
    in_specs = (
        P(None, both), P(None, both), P(None, None, both), P(None, both), P(both),
        P(None, "blk"), P("blk"), P("blk"), P("blk"),
        P(None, "blk"), P(None, "blk"), P(None, "blk"), P(None, "blk"), P(None, "blk"), P(None, "blk"),
    )
    out_specs = (P(None, both), P(None, both), P(None, None, both))
    return jax.shard_map(
        per_device, mesh=mesh, in_specs=in_specs, out_specs=out_specs, check_vma=False
    )
```

profile of v0, /device:TPU:80, one launch (start us, length us, event | category | flops | bytes accessed | tf_op | source)
XLA Modules:
  0.0 101.1 jit_solution(3412747323733069984)
XLA Ops:
  0.6 0.0 copy-start.6
  0.6 1.3 %broadcast_in_dim.17.invd_ref = f32[1,768]{1,0:T(1,128)} reshape(f32[768]{0:T(1024)} %param.22) | data formatting | bytes 6144 | tf_op jit(solution)/shard_map/broadcast_in_dim | solution.py:418
  1.9 0.6 broadcast_in_dim.16.len_ref
  2.5 5.6 %prepare.1 = (f32[344,256]{1,0:T(8,128)}, f32[168,256]{1,0:T(8,128)}, f32[344,128]{1,0:T(8,128)}, f32[344,128]{1,0:T(8,128)}, f32[344,128]{1,0:T(8,128)}, /*index=5*/f32[344,128]{1,0:T(8,128)}, s32[8,768]{1,0:T(8,128)}) custom-call(s32[6,16]{1,0:T(8,128)} %send_ref.1, f32[55,256]{1,0:T(8,128)} %p_ref.1, f32[55,768]{1,0:T(8,128)} %vel_ref.3, ...), custom_call_target="tpu_custom_call" | custom-call | tf_op jit(solution)/shard_map/prepare/pallas_call | solution.py:421
  8.1 44.0 %collective-permute-start.1 = (f32[344,128]{1,0:T(8,128)}, f32[344,128]{1,0:T(8,128)S(1)}, u32[]{:S(2)}, u32[]{:S(2)}) collective-permute-start(f32[344,128]{1,0:T(8,128)} %get-tuple-element.13), channel_id=1, source_target_pairs={{0,240},{1,241},{2,242},{3,243},{4,244},{5,245},{6,246},{7,247},{8... | collective-permute-start | bytes 528392 | tf_op jit(solution)/shard_map/ppermute | solution.py:403
  52.1 2.0 %collective-permute-start = (f32[344,128]{1,0:T(8,128)}, f32[344,128]{1,0:T(8,128)S(1)}, u32[]{:S(2)}, u32[]{:S(2)}) collective-permute-start(f32[344,128]{1,0:T(8,128)} %get-tuple-element.12), channel_id=1, source_target_pairs={{0,16},{1,17},{2,18},{3,19},{4,20},{5,21},{6,22},{7,23},{8,24},{9,... | collective-permute-start | bytes 528392 | tf_op jit(solution)/shard_map/ppermute | solution.py:403
  54.1 2.1 %collective-permute-done.1.north_ref = f32[344,128]{1,0:T(8,128)S(1)} collective-permute-done((f32[344,128]{1,0:T(8,128)}, f32[344,128]{1,0:T(8,128)S(1)}, u32[]{:S(2)}, u32[]{:S(2)}) %collective-permute-start.1) | collective-permute-done | bytes 176160 | tf_op jit(solution)/shard_map/ppermute | solution.py:403
  56.2 0.1 fusion.2
  56.3 0.6 copy-done
  56.9 0.1 fusion
  57.0 4.4 %collective-permute-done.south_ref = f32[344,128]{1,0:T(8,128)S(1)} collective-permute-done((f32[344,128]{1,0:T(8,128)}, f32[344,128]{1,0:T(8,128)S(1)}, u32[]{:S(2)}, u32[]{:S(2)}) %collective-permute-start) | collective-permute-done | bytes 176160 | tf_op jit(solution)/shard_map/ppermute | solution.py:403
  61.4 0.1 fusion.3
  61.6 0.5 copy-done.1
  62.1 0.1 fusion.1
  62.3 0.9 copy-done.5
  63.2 0.3 concatenate.7
  63.5 3.2 %collective-permute-start.3 = (f32[344,256]{1,0:T(8,128)S(1)}, f32[344,256]{1,0:T(8,128)S(1)}, u32[]{:S(2)}, u32[]{:S(2)}) collective-permute-start(f32[344,256]{1,0:T(8,128)S(1)} %concatenate.7), channel_id=1, source_target_pairs={{0,255},{1,0},{2,1},{3,2},{4,3},{5,4},{6,5},{7,6},{8,7},{9,8},{10,... | collective-permute-start | bytes 1056776 | tf_op jit(solution)/shard_map/ppermute | solution.py:403
  66.7 0.0 copy-done.4
  66.8 0.3 concatenate.6
  67.1 2.0 %collective-permute-start.2 = (f32[344,256]{1,0:T(8,128)S(1)}, f32[344,256]{1,0:T(8,128)S(1)}, u32[]{:S(2)}, u32[]{:S(2)}) collective-permute-start(f32[344,256]{1,0:T(8,128)S(1)} %concatenate.6), channel_id=1, source_target_pairs={{0,1},{1,2},{2,3},{3,4},{4,5},{5,6},{6,7},{7,8},{8,9},{9,10},{10,1... | collective-permute-start | bytes 1056776 | tf_op jit(solution)/shard_map/ppermute | solution.py:403
  69.1 2.5 %collective-permute-done.3.east_ref = f32[344,256]{1,0:T(8,128)S(1)} collective-permute-done((f32[344,256]{1,0:T(8,128)S(1)}, f32[344,256]{1,0:T(8,128)S(1)}, u32[]{:S(2)}, u32[]{:S(2)}) %collective-permute-start.3) | collective-permute-done | bytes 352288 | tf_op jit(solution)/shard_map/ppermute | solution.py:403
  71.6 7.5 %collective-permute-done.2.west_ref = f32[344,256]{1,0:T(8,128)S(1)} collective-permute-done((f32[344,256]{1,0:T(8,128)S(1)}, f32[344,256]{1,0:T(8,128)S(1)}, u32[]{:S(2)}, u32[]{:S(2)}) %collective-permute-start.2) | collective-permute-done | bytes 352288 | tf_op jit(solution)/shard_map/ppermute | solution.py:403
  79.1 0.7 copy-done.3
  79.8 21.2 %advance.1 = (f32[55,256]{1,0:T(8,128)}, f32[55,768]{1,0:T(8,128)}, f32[3,55,256]{2,1,0:T(8,128)}) custom-call(f32[344,256]{1,0:T(8,128)} %get-tuple-element.10.own_ref, f32[168,256]{1,0:T(8,128)} %get-tuple-element.11.trcl_ref, f32[344,128]{1,0:T(8,128)} %copy-done.1, f32[344,128]{1,0:T(8,128)} %copy-done, f32[344,256]{1,0:T(8,128)} %copy-done.3, ...), custom_call_target="tpu_custom_call" | custom-call | tf_op jit(solution)/shard_map/advance/pallas_call | solution.py:453
  (9 shorter events, 0.0 us)
Async XLA Ops:
  0.6 1.3 %copy-start.6 = (f32[768]{0:T(1024)S(1)}, f32[768]{0:T(1024)}, u32[]{:S(2)}) copy-start(f32[768]{0:T(1024)} %param.21) | copy-start | bytes 9220
  8.1 48.1 %collective-permute-start.1 = (f32[344,128]{1,0:T(8,128)}, f32[344,128]{1,0:T(8,128)S(1)}, u32[]{:S(2)}, u32[]{:S(2)}) collective-permute-start(f32[344,128]{1,0:T(8,128)} %get-tuple-element.13), channel_id=1, source_target_pairs={{0,240},{1,241},{2,242},{3,243},{4,244},{5,245},{6,246},{7,247},{8... | collective-permute-start | bytes 528392 | tf_op jit(solution)/shard_map/ppermute | solution.py:403
  52.1 9.3 %collective-permute-start = (f32[344,128]{1,0:T(8,128)}, f32[344,128]{1,0:T(8,128)S(1)}, u32[]{:S(2)}, u32[]{:S(2)}) collective-permute-start(f32[344,128]{1,0:T(8,128)} %get-tuple-element.12), channel_id=1, source_target_pairs={{0,16},{1,17},{2,18},{3,19},{4,20},{5,21},{6,22},{7,23},{8,24},{9,... | collective-permute-start | bytes 528392 | tf_op jit(solution)/shard_map/ppermute | solution.py:403
  56.2 0.7 copy-start
  61.4 0.7 copy-start.1
  62.3 0.9 copy-start.5
  63.2 3.6 %copy-start.4 = (f32[344,128]{1,0:T(8,128)S(1)}, f32[344,128]{1,0:T(8,128)}, u32[]{:S(2)}) copy-start(f32[344,128]{1,0:T(8,128)} %get-tuple-element.14) | copy-start | bytes 528388
  63.5 8.1 %collective-permute-start.3 = (f32[344,256]{1,0:T(8,128)S(1)}, f32[344,256]{1,0:T(8,128)S(1)}, u32[]{:S(2)}, u32[]{:S(2)}) collective-permute-start(f32[344,256]{1,0:T(8,128)S(1)} %concatenate.7), channel_id=1, source_target_pairs={{0,255},{1,0},{2,1},{3,2},{4,3},{5,4},{6,5},{7,6},{8,7},{9,8},{10,... | collective-permute-start | bytes 1056776 | tf_op jit(solution)/shard_map/ppermute | solution.py:403
  67.1 12.0 %collective-permute-start.2 = (f32[344,256]{1,0:T(8,128)S(1)}, f32[344,256]{1,0:T(8,128)S(1)}, u32[]{:S(2)}, u32[]{:S(2)}) collective-permute-start(f32[344,256]{1,0:T(8,128)S(1)} %concatenate.6), channel_id=1, source_target_pairs={{0,1},{1,2},{2,3},{3,4},{4,5},{5,6},{6,7},{7,8},{8,9},{9,10},{10,1... | collective-permute-start | bytes 1056776 | tf_op jit(solution)/shard_map/ppermute | solution.py:403
  71.6 7.5 %copy-start.2 = (f32[344,256]{1,0:T(8,128)}, f32[344,256]{1,0:T(8,128)S(1)}, u32[]{:S(2)}) copy-start(f32[344,256]{1,0:T(8,128)S(1)} %collective-permute-done.3.east_ref) | copy-start | bytes 1056772
  79.1 0.7 copy-start.3
where the time goes:
time: 101 us
  starting transfers between devices  51.1 us (51%)
  Pallas kernels  26.8 us (27%)
  waiting for transfers between devices  16.6 us (16%)
  local copies, waits for them, and re-layouts  5.81 us (6%)
    ppermute x4, starting transfers between devices, passed_along(): return lax.ppermute(value, axis, pairs)  51.1 us
    pallas_call x1, Pallas kernels, per_device(): pl.pallas_call(advance, out_shape=(shape((levels, CELLS), F32), shape((le...  21.2 us
    ppermute x4, waiting for transfers between devices, passed_along(): return lax.ppermute(value, axis, pairs)  16.6 us
    pallas_call x1, Pallas kernels, per_device(): pl.pallas_call(prepare, out_shape=(shape((rows, CELLS), F32), shape((trow...  5.58 us
    unnamed x14, local copies, waits for them, and re-layouts  2.76 us
  transfers between devices with their start and end apart: 4, of which 4 were waited for; matrix products, arithmetic and copies ran while one was open for 1% of the time, Pallas kernels for 0%

commit v1 on v0

--- a/solution.py
+++ b/solution.py
@@ -64,24 +64,37 @@
     return out
 
 
+def flat(ref):
+    return ref[...].reshape(1, ref.shape[0])
+
+
 def sixth(j):
     return (j * 43) >> 8
 
 
-def prepare(
-    send_ref, p_ref, vel_ref, trc_ref, tend_ref, pat_ref, coup_ref, len_ref, invd_ref, ia_ref, ends_ref,
-    own_ref, trcl_ref, up_ref, dn_ref, east_ref, west_ref, meta_ref,
-    x_ref, v_ref,
-):
+def prepare(*refs):
+    sources, rest = refs[:11], refs[11:]
+    own_ref, trcl_ref, up_ref, dn_ref, east_ref, west_ref, meta_ref, x_ref, v_ref = rest[:9]
+    send_ref, ends_ref, p_ref, vel_ref, trc_ref, tend_ref, pat_ref, coup_ref, len_ref, invd_ref, ia_ref = rest[9:20]
+    arrived = rest[20]
+    copies = [pltpu.make_async_copy(src, dst, arrived.at[n]) for n, (src, dst) in enumerate(zip(sources, rest[9:20]))]
+    for copy in copies:
+        copy.start()
+    copies[0].wait()
+    copies[1].wait()
     levels = p_ref.shape[0]
     edges = vel_ref.shape[1]
     start = ends_ref[0:1, :]
     end = ends_ref[1:2, :]
     start_hot = one_hot(start, CELLS)
     end_hot = one_hot(end, CELLS)
-    adjacent = dot_t(
+    joined = dot_t(
         jnp.concatenate([start_hot, end_hot], axis=1), jnp.concatenate([end_hot, start_hot], axis=1)
-    ).astype(BF16)
+    )
+    same = iota((CELLS, CELLS), 0) == iota((CELLS, CELLS), 1)
+    step1 = jnp.where(same, 1.0, jnp.minimum(1.0, joined)).astype(BF16)
+    step2 = jnp.minimum(1.0, dot(step1, step1)).astype(BF16)
+    step4 = jnp.minimum(1.0, dot(step2, step2)).astype(BF16)
     cell = iota((1, CELLS), 1)
     seeds = []
     for side in (1, 0, 3, 2):
@@ -90,10 +103,12 @@
             hit = hit | (cell == send_ref[side, s])
         seeds.append(jnp.where(hit, 1.0, 0.0))
     reached = rows8(*seeds)
-    far = 1.0 - reached
-    for _ in range(SIDE // 2 - 1):
-        reached = jnp.minimum(1.0, reached + dot(reached.astype(BF16), adjacent))
-        far = far + (1.0 - reached)
+    for step in (step1, step2, step4):
+        wider = jnp.minimum(1.0, dot(reached.astype(BF16), step))
+        reached = jnp.concatenate([reached, wider], axis=0)
+    far = jnp.zeros((8, CELLS), F32)
+    for n in range(SIDE // 2):
+        far = far + (1.0 - reached[8 * n : 8 * n + 8])
     half = SIDE // 2
     a = jnp.where(far[0:1] < half, far[0:1], SIDE - 1.0 - far[1:2])
     b = jnp.where(far[2:3] < half, far[2:3], SIDE - 1.0 - far[3:4])
@@ -125,13 +140,15 @@
     meta = jnp.where(at8 == 0, spot, jnp.where(at8 == 1, sense.astype(I32), zero))
     meta_ref[...] = meta
     meta_ref[2:3, 0:CELLS] = place
+    for copy in copies[2:]:
+        copy.wait()
     x_ref[...] = jnp.zeros(x_ref.shape, F32)
     height = iota((levels, 1), 0).astype(F32)
     taper = jnp.minimum(1.0, (levels - 1.0 - height) / (0.25 * levels))
     x_ref[0:levels] = p_ref[...]
-    x_ref[GROUP : GROUP + levels] = force_scale * (1.0 + pat_ref[...] * taper) * tend_ref[...]
+    x_ref[GROUP : GROUP + levels] = force_scale * (1.0 + flat(pat_ref) * taper) * tend_ref[...]
     x_ref[2 * GROUP : 2 * GROUP + levels] = coup_ref[...]
-    x_ref[3 * GROUP : 3 * GROUP + 1] = ia_ref[...]
+    x_ref[3 * GROUP : 3 * GROUP + 1] = flat(ia_ref)
     first = 3 * GROUP + 8
     for n in range(trc_ref.shape[0]):
         x_ref[first + n * GROUP : first + n * GROUP + levels] = trc_ref[n]
@@ -141,8 +158,8 @@
     trcl_ref[...] = moved[first:]
     v_ref[...] = jnp.zeros(v_ref.shape, F32)
     v_ref[0:levels] = vel_ref[...] * sense
-    v_ref[GROUP : GROUP + 1] = len_ref[...]
-    v_ref[GROUP + 1 : GROUP + 2] = invd_ref[...]
+    v_ref[GROUP : GROUP + 1] = flat(len_ref)
+    v_ref[GROUP + 1 : GROUP + 2] = flat(invd_ref)
     v_hi, v_lo = halves(v_ref[...])
     lengths, distances = [], []
     for k in range(3):
@@ -176,10 +193,30 @@
         ref[rims.shape[0] :] = rest[:, 128 * number : 128 * number + 128]
 
 
+def pack(east_ref, west_ref, south_ref, north_ref, to_east_ref, to_west_ref):
+    rows = east_ref.shape[0]
+    split = rows - to_east_ref.shape[0]
+    cut = DEPTH * DEPTH
+    wide = DEPTH * SIDE
+    rim = wide + SIDE
+    for part, out, body, corner in (
+        (east_ref, to_east_ref, wide - cut, rim - 1), (west_ref, to_west_ref, 0, wide),
+    ):
+        out[split:, 0:256] = jnp.zeros((out.shape[0] - split, 256), F32)
+        for begin, end, at in ((0, split, 0), (split, rows, 192)):
+            count = end - begin
+            line = [
+                part[begin:end, 0:rim], south_ref[begin:end, body : body + cut],
+                north_ref[begin:end, body : body + cut], south_ref[begin:end, corner : corner + 1],
+                north_ref[begin:end, corner : corner + 1], jnp.zeros((count, 6), F32),
+            ]
+            out[0:count, at : at + 192] = jnp.concatenate(line, axis=1)
+
+
 def advance(
     own_ref, trcl_ref, south_ref, north_ref, west_ref, east_ref, meta_ref, vel_ref, invd_ref,
     newp_ref, newv_ref, newt_ref,
-    big_ref, trc_ref, hist_ref, t_ref, f_ref, inv_ref, al_ref, be_ref, out_ref, dq_ref,
+    big_ref, trc_ref, hist_ref, t_ref, f_ref, inv_ref, al_ref, be_ref, out_ref, dq_ref, flow_ref,
 ):
     levels = newp_ref.shape[0]
     species = newt_ref.shape[0]
@@ -192,18 +229,15 @@
     inside = (qb >= 0) & (qb < SIDE)
     below = (qb >= -DEPTH) & (qb < 0)
     above = (qb >= SIDE) & (qb < SIDE + DEPTH)
-    src = jnp.where(
-        inside, qa * SIDE + qb,
-        jnp.where(below, 256 + qa * DEPTH + qb + DEPTH, jnp.where(above, 384 + qa * DEPTH + qb - SIDE, -1)),
-    )
-    tsrc = jnp.where(
-        inside, qa * SIDE + qb, jnp.where(qb == -1, 256 + 96 + qa, jnp.where(qb == SIDE, 384 + 96 + qa, -1))
-    )
-    s_val, n_val = south_ref[...], north_ref[...]
-    core = pick(jnp.concatenate([own_ref[...], s_val, n_val], axis=1), one_hot(src, 512))
-    tcore = pick(
-        jnp.concatenate([trcl_ref[...], s_val[0:trows], n_val[0:trows]], axis=1), one_hot(tsrc, 512)
-    )
+    src = jnp.where(inside, qa * SIDE + qb, -1)
+    rsrc = jnp.where(below, qa * DEPTH + qb + DEPTH, jnp.where(above, 128 + qa * DEPTH + qb - SIDE, -1))
+    tsrc = jnp.where(qb == -1, 96 + qa, jnp.where(qb == SIDE, 128 + 96 + qa, -1))
+    sn_hi, sn_lo = halves(jnp.concatenate([south_ref[...], north_ref[...]], axis=1))
+    own_hot = one_hot(src, 256)
+    rim_hot = one_hot(rsrc, 256)
+    core = pick(own_ref[...], own_hot) + (dot(sn_hi, rim_hot) + dot(sn_lo, rim_hot))
+    rim_hot = one_hot(tsrc, 256)
+    tcore = pick(trcl_ref[...], own_hot) + (dot(sn_hi[0:trows], rim_hot) + dot(sn_lo[0:trows], rim_hot))
     for s in range(4):
         big_ref[pl.ds(2 + s, rows, stride=8), :] = core[:, 128 * s : 128 * s + 128]
         trc_ref[pl.ds(2 + s, trows, stride=8), :] = tcore[:, 128 * s : 128 * s + 128]
@@ -227,36 +261,31 @@
         hi, lo = halves(ref[...])
         hot = one_hot(src, 256)
         thot = one_hot(tsrc, 256)
-        flank = dot(hi, hot) + dot(lo, hot)
-        tflank = dot(hi[0:trows], thot) + dot(lo[0:trows], thot)
+        late_hot = one_hot(jnp.where(src >= 0, src + 64, -1), 256)
+        flank = dot(hi[0:trows, 0:256], hot) + dot(lo[0:trows, 0:256], hot)
+        late = dot(hi[:, 128:384], late_hot) + dot(lo[:, 128:384], late_hot)
+        tflank = dot(hi[0:trows, 0:256], thot) + dot(lo[0:trows, 0:256], thot)
         for s in range(2):
-            big_ref[pl.ds(side + s, rows, stride=8), :] = flank[:, 128 * s : 128 * s + 128]
-            trc_ref[pl.ds(side + s, trows, stride=8), :] = tflank[:, 128 * s : 128 * s + 128]
+            cut = slice(128 * s, 128 * s + 128)
+            big_ref[pl.ds(side + s, trows, stride=8), :] = flank[:, cut]
+            big_ref[pl.ds(8 * trows + side + s, rows - trows, stride=8), :] = late[:, cut]
+            trc_ref[pl.ds(side + s, trows, stride=8), :] = tflank[:, cut]
 
     lane = iota((8, 128), 1)
-    first_group = lane < COL
-    last_group = lane >= 128 - COL
-
-    def b_up(x):
-        return pltpu.roll(x, 127, 1)
-
-    def b_dn(x):
-        return pltpu.roll(x, 1, 1)
-
-    def a_up(x):
-        y = pltpu.roll(x, 128 - COL, 1)
-        return jnp.where(last_group, pltpu.roll(y, 7, 0), y)
-
-    def a_dn(x):
-        y = pltpu.roll(x, COL, 1)
-        return jnp.where(first_group, pltpu.roll(y, 1, 0), y)
+
+    def ahead(x, step):
+        y = pltpu.roll(x, 128 - step, 1)
+        return jnp.where(lane >= 128 - step, pltpu.roll(y, 7, 0), y)
+
+    def behind(x, step):
+        y = pltpu.roll(x, step, 1)
+        return jnp.where(lane < step, pltpu.roll(y, 1, 0), y)
 
     def ups(x):
-        right = a_up(x)
-        return right, b_up(x), b_dn(right)
+        return ahead(x, COL), pltpu.roll(x, 127, 1), ahead(x, COL - 1)
 
     def back(x0, x1, x2):
-        return a_dn(x0), b_dn(x1), b_up(a_dn(x2))
+        return behind(x0, COL), pltpu.roll(x1, 1, 1), behind(x2, COL - 1)
 
     def row(ref, number):
         return ref[8 * number : 8 * number + 8, :]
@@ -283,7 +312,7 @@
         hist_ref[at, :] = dyn(big_ref, l)
         return carry
 
-    lax.fori_loop(0, levels, first_spread, 0, unroll=5)
+    lax.fori_loop(0, levels, first_spread, 0, unroll=55)
 
     middle = levels // 2
     c = [row(big_ref, 2 * GROUP + l) for l in range(levels)] + [jnp.zeros((8, 128), F32)]
@@ -314,26 +343,27 @@
 
         def source(l):
             p = hist_ref[pl.ds(pl.multiple_of(here + 8 * l, 8), 8), :]
-            right = a_up(p)
-            left = a_dn(p)
+            fore = ups(p)
+            rear = back(p, p, p)
             t = row(t_ref, l) + mid_coef * p
-            t = t + (out_coef[0] * right + in_coef[0] * left)
-            t = t + (out_coef[1] * b_up(p) + in_coef[1] * b_dn(p))
-            t = t + (out_coef[2] * b_dn(right) + in_coef[2] * b_up(left))
+            for k in range(3):
+                t = t + (out_coef[k] * fore[k] + in_coef[k] * rear[k])
             t_ref[8 * l : 8 * l + 8, :] = t
-            return (p + t) * row(inv_ref, l)
+            f_ref[8 * l : 8 * l + 8, :] = (p + t) * row(inv_ref, l)
 
         def put(l, value):
             hist_ref[pl.ds(pl.multiple_of(there + 8 * l, 8), 8), :] = value
 
-        low = high = None
-        for l in range(middle):
+        for l in range(levels):
+            source(l)
+        low, high = row(f_ref, 0), row(f_ref, levels - 1)
+        for l in range(1, middle):
             h = levels - 1 - l
-            low = source(l) if low is None else source(l) + row(al_ref, l) * low
-            high = source(h) if high is None else source(h) + row(be_ref, h) * high
+            low = row(f_ref, l) + row(al_ref, l) * low
+            high = row(f_ref, h) + row(be_ref, h) * high
             f_ref[8 * l : 8 * l + 8, :] = low
             f_ref[8 * h : 8 * h + 8, :] = high
-        low = high = source(middle) + row(al_ref, middle) * low + row(be_ref, middle) * high
+        low = high = row(f_ref, middle) + row(al_ref, middle) * low + row(be_ref, middle) * high
         put(middle, low)
         for l in range(middle - 1, -1, -1):
             h = levels - 1 - l
@@ -357,29 +387,49 @@
             total = p if total is None else total + p
             weighted = total if weighted is None else weighted + total
         out_ref[at, :] = hist_ref[pl.ds(pl.multiple_of(8 * (levels * SUBSTEPS + l), 8), 8), :]
-        toward, away = [], []
         shifted = ups(total)
         weight_shift = ups(weighted)
         for k in range(3):
             dq_ref[pl.ds(pl.multiple_of(8 * (GROUP * k + l), 8), 8), :] = shifted[k] - total
             mean = dyn(big_ref, (3 + k) * GROUP + l) - scale[k] * (weight_shift[k] - weighted)
-            toward.append(length[k] * jnp.maximum(mean, 0.0))
-            away.append(length[k] * jnp.minimum(mean, 0.0))
+            flow_ref[pl.ds(pl.multiple_of(8 * (GROUP * k + l), 8), 8), :] = length[k] * jnp.maximum(mean, 0.0)
+            flow_ref[pl.ds(pl.multiple_of(8 * (GROUP * (3 + k) + l), 8), 8), :] = length[k] * jnp.minimum(mean, 0.0)
+        return carry
+
+    lax.fori_loop(0, levels, finish, 0, unroll=55)
+
+    def carry_tracers(l, carry):
+        toward = [dyn(flow_ref, GROUP * k + l) for k in range(3)]
+        away = [dyn(flow_ref, GROUP * (3 + k) + l) for k in range(3)]
+        toward_in = back(*toward)
+        away_in = back(*away)
+        keep = (toward[0] - away_in[0]) + (toward[1] - away_in[1]) + (toward[2] - away_in[2])
         for s in range(species):
             tr = dyn(trc_ref, s * GROUP + l)
             beyond = ups(tr)
-            flux = [toward[k] * tr + away[k] * beyond[k] for k in range(3)]
-            flux_in = back(*flux)
-            spread = (flux[0] - flux_in[0]) + (flux[1] - flux_in[1]) + (flux[2] - flux_in[2])
+            before = back(tr, tr, tr)
+            spread = keep * tr
+            for k in range(3):
+                spread = spread + (away[k] * beyond[k] - toward_in[k] * before[k])
             out_ref[pl.ds(pl.multiple_of(8 * ((s + 1) * GROUP + l), 8), 8), :] = tr - drain * spread
         return carry
 
-    lax.fori_loop(0, levels, finish, 0, unroll=5)
-
-    place = meta_ref[2:3, 0:CELLS]
-    spot = ((place >> 4) << 5) + (place & 15) + DEPTH
-    cells = jnp.concatenate([out_ref[pl.ds(2 + s, 4 * GROUP, stride=8), :] for s in range(4)], axis=1)
-    cells = pick(cells, one_hot(spot, 512))
+    lax.fori_loop(0, levels, carry_tracers, 0, unroll=55)
+
+    kept = (iota((1, 128), 1) & 31) - DEPTH
+    kept = (kept >= 0) & (kept < SIDE)
+
+    def folded(ref, begin, count):
+        blocks = [ref[pl.ds(8 * begin + 2 + s, count, stride=8), :] for s in range(4)]
+        pairs = [jnp.where(kept, blocks[s], pltpu.roll(blocks[s + 1], SIDE, 1)) for s in (0, 2)]
+        return jnp.concatenate(pairs, axis=1)
+
+    def lane_of(place):
+        column = place >> 4
+        at = ((column & 3) << 5) + (place & 15) + DEPTH + ((column >> 2) & 1) * SIDE
+        return ((column >> 3) << 7) + (at & 127)
+
+    cells = pick(folded(out_ref, 0, 4 * GROUP), one_hot(lane_of(meta_ref[2:3, 0:CELLS]), 256))
     newp_ref[...] = cells[0:levels]
     for s in range(species):
         newt_ref[s] = cells[(s + 1) * GROUP : (s + 1) * GROUP + levels]
@@ -387,14 +437,10 @@
     turned = jnp.zeros((GROUP, edges), F32)
     for k in range(3):
         place = spot - k * CELLS
-        lane_of = ((place >> 4) << 5) + (place & 15) + DEPTH
-        lane_of = jnp.where((place >= 0) & (place < CELLS), lane_of, -1)
-        part = jnp.concatenate(
-            [dq_ref[pl.ds(8 * GROUP * k + 2 + s, GROUP, stride=8), :] for s in range(4)], axis=1
-        )
-        turned = turned + pick(part, one_hot(lane_of, 512))
+        at = jnp.where((place >= 0) & (place < CELLS), lane_of(place & (CELLS - 1)), -1)
+        turned = turned + pick(folded(dq_ref, GROUP * k, GROUP), one_hot(at, 256))
     sense = meta_ref[1:2, :].astype(F32)
-    newv_ref[...] = vel_ref[...] - (grad_scale * sense * invd_ref[...]) * turned[0:levels]
+    newv_ref[...] = vel_ref[...] - (grad_scale * sense * flat(invd_ref)) * turned[0:levels]
 
 
 def passed_along(value, axis, steps):
@@ -415,9 +461,13 @@
     stride = lax.axis_size("blk") // 16
     rows = 6 * GROUP + 8
     trows = species * GROUP
-    invd_row = inv_distance[None, :]
     shape = jax.ShapeDtypeStruct
     vmem = pl.BlockSpec(memory_space=pltpu.VMEM)
+    inputs = (
+        cell_send, edge_ends, pressure, velocity, tracers, tendency, pattern, coupling, edge_length,
+        inv_distance, inv_area,
+    )
+    inputs = [pltpu.with_memory_space_constraint(array, pltpu.HBM) for array in inputs]
     own, trc, up, down, east, west, meta = pl.pallas_call(
         prepare,
         out_shape=(
@@ -425,28 +475,28 @@
             shape((rows, 128), F32), shape((rows, 128), F32), shape((rows, 128), F32), shape((rows, 128), F32),
             shape((8, edges), I32),
         ),
-        in_specs=[pl.BlockSpec(memory_space=pltpu.SMEM)] + [vmem] * 10,
+        in_specs=[pl.BlockSpec(memory_space=pltpu.HBM)] * 11,
         out_specs=(vmem,) * 7,
-        scratch_shapes=[pltpu.VMEM((3 * GROUP + 8 + trows, CELLS), F32), pltpu.VMEM((GROUP + 8, edges), F32)],
+        scratch_shapes=[
+            pltpu.VMEM((3 * GROUP + 8 + trows, CELLS), F32), pltpu.VMEM((GROUP + 8, edges), F32),
+            pltpu.SMEM(cell_send.shape, I32),
+        ] + [pltpu.VMEM(array.shape, array.dtype) for array in inputs[1:]] + [pltpu.SemaphoreType.DMA((11,))],
+        compiler_params=pltpu.CompilerParams(vmem_limit_bytes=40 * 2**20),
         interpret=INTERPRET,
         name="prepare",
-    )(
-        cell_send, pressure, velocity, tracers, tendency, pattern[None, :], coupling, edge_length[None, :],
-        invd_row, inv_area[None, :], edge_ends,
-    )
+    )(*inputs)
     south = passed_along(up, "blk", stride)
     north = passed_along(down, "blk", -stride)
-    blank = jnp.zeros((rows, 70), F32)
-    cut = DEPTH * DEPTH
-    wide = DEPTH * SIDE
-    to_east = jnp.concatenate(
-        [east[:, :112], south[:, wide - cut : wide], north[:, wide - cut : wide],
-         south[:, wide + 15 : wide + 16], north[:, wide + 15 : wide + 16], blank], axis=1,
-    )
-    to_west = jnp.concatenate(
-        [west[:, :112], south[:, :cut], north[:, :cut],
-         south[:, wide : wide + 1], north[:, wide : wide + 1], blank], axis=1,
-    )
+    half = shape((rows - trows, 384), F32)
+    to_east, to_west = pl.pallas_call(
+        pack,
+        out_shape=(half, half),
+        in_specs=[vmem] * 4,
+        out_specs=(vmem,) * 2,
+        compiler_params=pltpu.CompilerParams(vmem_limit_bytes=40 * 2**20),
+        interpret=INTERPRET,
+        name="pack",
+    )(east, west, south, north)
     from_west = passed_along(to_east, "blk", 1)
     from_east = passed_along(to_west, "blk", -1)
     block = pltpu.VMEM((levels * 8, 128), F32)
@@ -462,10 +512,12 @@
             pltpu.VMEM(((SUBSTEPS + 1) * levels * 8, 128), F32),
             block, block, block, block, block,
             pltpu.VMEM((4 * GROUP * 8, 128), F32), pltpu.VMEM((3 * GROUP * 8, 128), F32),
+            pltpu.VMEM((6 * GROUP * 8, 128), F32),
         ],
+        compiler_params=pltpu.CompilerParams(vmem_limit_bytes=40 * 2**20),
         interpret=INTERPRET,
         name="advance",
-    )(own, trc, south, north, from_west, from_east, meta, velocity, invd_row)
+    )(own, trc, south, north, from_west, from_east, meta, velocity, inv_distance)
 
 
 def solution(mesh):

time: 101 us -> 77.3 us (0.77)
  Pallas kernels: 26.8 us -> 12.6 us
  waiting for transfers between devices: 16.6 us -> 7.72 us
  local copies, waits for them, and re-layouts: 5.81 us -> 0.01 us
  starting transfers between devices: 51.1 us -> 55.5 us
    pallas_call x1, Pallas kernels: 21.2 us -> 7.64 us  [per_device(): pl.pallas_call(advance, out_shape=(shape((levels, CELLS), F32), shape((le...]
    ppermute x4, waiting for transfers between devices: 16.6 us -> 7.72 us  [passed_along(): return lax.ppermute(value, axis, pairs)]
    ppermute x4, starting transfers between devices: 51.1 us -> 55.5 us  [passed_along(): return lax.ppermute(value, axis, pairs)]
    unnamed x14 -> x4, local copies, waits for them, and re-layouts: 2.76 us -> 0.01 us
    broadcast_in_dim x3 -> x0, local copies, waits for them, and re-layouts: 1.88 us -> none  [the longest x1 1.28 us: per_device(): invd_row = inv_distance[None, :]]
    pallas_call x1, Pallas kernels: 5.58 us -> 4.38 us  [per_device(): pl.pallas_call(prepare, out_shape=(shape((rows, CELLS), F32), shape((trow...]
  transfers between devices with their start and end apart: 4 -> 4, of which waited for: 4 -> 4; matrix products, arithmetic and copies ran while one was open for 1% -> 0% of each run, Pallas kernels for 0% -> 0%
where the time goes in v1:
time: 77.3 us; the launch traced here: 76.5 us
  starting transfers between devices  55.5 us (72%)
  Pallas kernels  12.6 us (16%)
  waiting for transfers between devices  7.72 us (10%)
    ppermute x4, starting transfers between devices, passed_along(): return lax.ppermute(value, axis, pairs)  55.5 us
    ppermute x4, waiting for transfers between devices, passed_along(): return lax.ppermute(value, axis, pairs)  7.72 us
    pallas_call x1, Pallas kernels, per_device(): pl.pallas_call(advance, out_shape=(shape((levels, CELLS), F32), shape((le...  7.64 us
    pallas_call x1, Pallas kernels, per_device(): pl.pallas_call(prepare, out_shape=(shape((rows, CELLS), F32), shape((trow...  4.38 us
  transfers between devices with their start and end apart: 4, of which 4 were waited for; matrix products, arithmetic and copies ran while one was open for 0% of the time, Pallas kernels for 0%

profile of v1, /device:TPU:80, one launch (start us, length us, event | category | flops | bytes accessed | tf_op | source)
XLA Modules:
  0.0 76.5 jit_solution(5333893747461541254)
XLA Ops:
  0.6 4.4 %prepare.1 = (f32[344,256]{1,0:T(8,128)S(1)}, f32[168,256]{1,0:T(8,128)S(1)}, f32[344,128]{1,0:T(8,128)S(1)}, f32[344,128]{1,0:T(8,128)S(1)}, f32[344,128]{1,0:T...) custom-call(s32[6,16]{1,0:T(8,128)} %refs_0_.1, s32[2,768]{1,0:T(2,128)} %refs_1_.1, f32[55,256]{1,0:T(8,128)} %refs_2_.1, ...), custom_call_target="tpu_custom_call" | custom-call | tf_op jit(solution)/shard_map/prepare/pallas_call | solution.py:471
  5.0 6.0 %collective-permute-start = (f32[344,128]{1,0:T(8,128)S(1)}, f32[344,128]{1,0:T(8,128)S(1)}, u32[]{:S(2)}, u32[]{:S(2)}) collective-permute-start(f32[344,128]{1,0:T(8,128)S(1)} %get-tuple-element.14), channel_id=1, source_target_pairs={{0,16},{1,17},{2,18},{3,19},{4,20},{5,21},{6,22},{7,23},{8,24},{9,... | collective-permute-start | bytes 528392 | tf_op jit(solution)/shard_map/ppermute | solution.py:449
  11.1 39.9 %collective-permute-start.1 = (f32[344,128]{1,0:T(8,128)S(1)}, f32[344,128]{1,0:T(8,128)S(1)}, u32[]{:S(2)}, u32[]{:S(2)}) collective-permute-start(f32[344,128]{1,0:T(8,128)S(1)} %get-tuple-element.15), channel_id=1, source_target_pairs={{0,240},{1,241},{2,242},{3,243},{4,244},{5,245},{6,246},{7,247},{8... | collective-permute-start | bytes 528392 | tf_op jit(solution)/shard_map/ppermute | solution.py:449
  51.0 2.6 %collective-permute-done.south_ref = f32[344,128]{1,0:T(8,128)S(1)} collective-permute-done((f32[344,128]{1,0:T(8,128)S(1)}, f32[344,128]{1,0:T(8,128)S(1)}, u32[]{:S(2)}, u32[]{:S(2)}) %collective-permute-start) | collective-permute-done | bytes 176160 | tf_op jit(solution)/shard_map/ppermute | solution.py:449
  53.6 1.2 %collective-permute-done.1.north_ref = f32[344,128]{1,0:T(8,128)S(1)} collective-permute-done((f32[344,128]{1,0:T(8,128)S(1)}, f32[344,128]{1,0:T(8,128)S(1)}, u32[]{:S(2)}, u32[]{:S(2)}) %collective-permute-start.1) | collective-permute-done | bytes 176160 | tf_op jit(solution)/shard_map/ppermute | solution.py:449
  54.8 0.0 copy-start
  54.8 0.6 pack.1
  55.4 0.0 copy-start.1
  55.4 2.0 %collective-permute-start.2 = (f32[176,384]{1,0:T(8,128)S(1)}, f32[176,384]{1,0:T(8,128)S(1)}, u32[]{:S(2)}, u32[]{:S(2)}) collective-permute-start(f32[176,384]{1,0:T(8,128)S(1)} %get-tuple-element.18), channel_id=1, source_target_pairs={{0,1},{1,2},{2,3},{3,4},{4,5},{5,6},{6,7},{7,8},{8,9},{9,10},{10,1... | collective-permute-start | bytes 811016 | tf_op jit(solution)/shard_map/ppermute | solution.py:449
  57.4 7.5 %collective-permute-start.3 = (f32[176,384]{1,0:T(8,128)S(1)}, f32[176,384]{1,0:T(8,128)S(1)}, u32[]{:S(2)}, u32[]{:S(2)}) collective-permute-start(f32[176,384]{1,0:T(8,128)S(1)} %get-tuple-element.19), channel_id=1, source_target_pairs={{0,255},{1,0},{2,1},{3,2},{4,3},{5,4},{6,5},{7,6},{8,7},{9,8},{10,... | collective-permute-start | bytes 811016 | tf_op jit(solution)/shard_map/ppermute | solution.py:449
  64.9 2.2 %collective-permute-done.2.west_ref = f32[176,384]{1,0:T(8,128)S(1)} collective-permute-done((f32[176,384]{1,0:T(8,128)S(1)}, f32[176,384]{1,0:T(8,128)S(1)}, u32[]{:S(2)}, u32[]{:S(2)}) %collective-permute-start.2) | collective-permute-done | bytes 270368 | tf_op jit(solution)/shard_map/ppermute | solution.py:449
  67.1 1.8 %collective-permute-done.3.east_ref = f32[176,384]{1,0:T(8,128)S(1)} collective-permute-done((f32[176,384]{1,0:T(8,128)S(1)}, f32[176,384]{1,0:T(8,128)S(1)}, u32[]{:S(2)}, u32[]{:S(2)}) %collective-permute-start.3) | collective-permute-done | bytes 270368 | tf_op jit(solution)/shard_map/ppermute | solution.py:449
  68.9 0.0 copy-done
  68.9 0.0 copy-done.1
  68.9 7.6 %advance.1 = (f32[55,256]{1,0:T(8,128)}, f32[55,768]{1,0:T(8,128)}, f32[3,55,256]{2,1,0:T(8,128)}) custom-call(f32[344,256]{1,0:T(8,128)S(1)} %get-tuple-element.12.own_ref, f32[168,256]{1,0:T(8,128)S(1)} %get-tuple-element.13.trcl_ref, f32[344,128]{1,0:T(8,128)S(1)} %collective-permute-done.south_ref, f32[344,128]{1,0:T(8,128)S(1)} %collective-permute-done.1.north_ref, ...), custom_call_target="tpu_custom_call" | custom-call | tf_op jit(solution)/shard_map/advance/pallas_call | solution.py:503
Async XLA Ops:
  5.0 48.5 %collective-permute-start = (f32[344,128]{1,0:T(8,128)S(1)}, f32[344,128]{1,0:T(8,128)S(1)}, u32[]{:S(2)}, u32[]{:S(2)}) collective-permute-start(f32[344,128]{1,0:T(8,128)S(1)} %get-tuple-element.14), channel_id=1, source_target_pairs={{0,16},{1,17},{2,18},{3,19},{4,20},{5,21},{6,22},{7,23},{8,24},{9,... | collective-permute-start | bytes 528392 | tf_op jit(solution)/shard_map/ppermute | solution.py:449
  11.1 43.7 %collective-permute-start.1 = (f32[344,128]{1,0:T(8,128)S(1)}, f32[344,128]{1,0:T(8,128)S(1)}, u32[]{:S(2)}, u32[]{:S(2)}) collective-permute-start(f32[344,128]{1,0:T(8,128)S(1)} %get-tuple-element.15), channel_id=1, source_target_pairs={{0,240},{1,241},{2,242},{3,243},{4,244},{5,245},{6,246},{7,247},{8... | collective-permute-start | bytes 528392 | tf_op jit(solution)/shard_map/ppermute | solution.py:449
  54.8 14.1 %copy-start = (f32[55,768]{1,0:T(8,128)S(1)}, f32[55,768]{1,0:T(8,128)}, u32[]{:S(2)}) copy-start(f32[55,768]{1,0:T(8,128)} %vel_ref.1) | copy-start | bytes 506884
  55.4 13.5 %copy-start.1 = (f32[768]{0:T(1024)S(1)}, f32[768]{0:T(1024)}, u32[]{:S(2)}) copy-start(f32[768]{0:T(1024)} %invd_ref.1) | copy-start | bytes 9220
  55.4 11.7 %collective-permute-start.2 = (f32[176,384]{1,0:T(8,128)S(1)}, f32[176,384]{1,0:T(8,128)S(1)}, u32[]{:S(2)}, u32[]{:S(2)}) collective-permute-start(f32[176,384]{1,0:T(8,128)S(1)} %get-tuple-element.18), channel_id=1, source_target_pairs={{0,1},{1,2},{2,3},{3,4},{4,5},{5,6},{6,7},{7,8},{8,9},{9,10},{10,1... | collective-permute-start | bytes 811016 | tf_op jit(solution)/shard_map/ppermute | solution.py:449
  57.4 11.5 %collective-permute-start.3 = (f32[176,384]{1,0:T(8,128)S(1)}, f32[176,384]{1,0:T(8,128)S(1)}, u32[]{:S(2)}, u32[]{:S(2)}) collective-permute-start(f32[176,384]{1,0:T(8,128)S(1)} %get-tuple-element.19), channel_id=1, source_target_pairs={{0,255},{1,0},{2,1},{3,2},{4,3},{5,4},{6,5},{7,6},{8,7},{9,8},{10,... | collective-permute-start | bytes 811016 | tf_op jit(solution)/shard_map/ppermute | solution.py:449

commit v2 on v1

--- a/solution.py
+++ b/solution.py
@@ -1,11 +1,10 @@
-import functools
-
 import jax
 import jax.numpy as jnp
 from jax import lax
 from jax.experimental import pallas as pl
 from jax.experimental.pallas import tpu as pltpu
 from jax.sharding import PartitionSpec as P
+
 
 SUBSTEPS = 6
 grad_scale = 0.25
@@ -213,15 +212,7 @@
             out[0:count, at : at + 192] = jnp.concatenate(line, axis=1)
 
 
-def advance(
-    own_ref, trcl_ref, south_ref, north_ref, west_ref, east_ref, meta_ref, vel_ref, invd_ref,
-    newp_ref, newv_ref, newt_ref,
-    big_ref, trc_ref, hist_ref, t_ref, f_ref, inv_ref, al_ref, be_ref, out_ref, dq_ref, flow_ref,
-):
-    levels = newp_ref.shape[0]
-    species = newt_ref.shape[0]
-    edges = newv_ref.shape[1]
-    rows = own_ref.shape[0]
+def settle(own_ref, trcl_ref, south_ref, north_ref, meta_ref, core_ref, tcore_ref, cell_hot_ref, edge_hot_ref):
     trows = trcl_ref.shape[0]
     q = iota((1, 512), 1)
     qa = q >> 5
@@ -235,12 +226,36 @@
     sn_hi, sn_lo = halves(jnp.concatenate([south_ref[...], north_ref[...]], axis=1))
     own_hot = one_hot(src, 256)
     rim_hot = one_hot(rsrc, 256)
-    core = pick(own_ref[...], own_hot) + (dot(sn_hi, rim_hot) + dot(sn_lo, rim_hot))
+    core_ref[...] = pick(own_ref[...], own_hot) + (dot(sn_hi, rim_hot) + dot(sn_lo, rim_hot))
     rim_hot = one_hot(tsrc, 256)
-    tcore = pick(trcl_ref[...], own_hot) + (dot(sn_hi[0:trows], rim_hot) + dot(sn_lo[0:trows], rim_hot))
+    tcore_ref[...] = pick(trcl_ref[...], own_hot) + (dot(sn_hi[0:trows], rim_hot) + dot(sn_lo[0:trows], rim_hot))
+
+    def lane_of(place):
+        column = place >> 4
+        at = ((column & 3) << 5) + (place & 15) + DEPTH + ((column >> 2) & 1) * SIDE
+        return ((column >> 3) << 7) + (at & 127)
+
+    cell_hot_ref[...] = one_hot(lane_of(meta_ref[2:3, 0:CELLS]), 256)
+    spot = meta_ref[0:1, :]
+    for k in range(3):
+        place = spot - k * CELLS
+        at = jnp.where((place >= 0) & (place < CELLS), lane_of(place & (CELLS - 1)), -1)
+        edge_hot_ref[256 * k : 256 * k + 256] = one_hot(at, 256)
+
+
+def advance(
+    core_ref, tcore_ref, west_ref, east_ref, cell_hot_ref, edge_hot_ref, meta_ref, vel_ref, invd_ref,
+    newp_ref, newv_ref, newt_ref,
+    big_ref, trc_ref, hist_ref, t_ref, f_ref, inv_ref, al_ref, be_ref, out_ref, dq_ref, flow_ref,
+):
+    levels = newp_ref.shape[0]
+    species = newt_ref.shape[0]
+    edges = newv_ref.shape[1]
+    rows = core_ref.shape[0]
+    trows = tcore_ref.shape[0]
     for s in range(4):
-        big_ref[pl.ds(2 + s, rows, stride=8), :] = core[:, 128 * s : 128 * s + 128]
-        trc_ref[pl.ds(2 + s, trows, stride=8), :] = tcore[:, 128 * s : 128 * s + 128]
+        big_ref[pl.ds(2 + s, rows, stride=8), :] = core_ref[:, 128 * s : 128 * s + 128]
+        trc_ref[pl.ds(2 + s, trows, stride=8), :] = tcore_ref[:, 128 * s : 128 * s + 128]
     q = iota((1, 256), 1)
     qb = (q & 31) - DEPTH
     inside = (qb >= 0) & (qb < SIDE)
@@ -373,7 +388,7 @@
             put(h, high)
         return carry
 
-    lax.fori_loop(0, SUBSTEPS, substep, 0)
+    lax.fori_loop(0, SUBSTEPS, substep, 0, unroll=True)
 
     scale = [g * (1.0 / SUBSTEPS) for g in grad]
     drain = tracer_scale * area
@@ -424,21 +439,13 @@
         pairs = [jnp.where(kept, blocks[s], pltpu.roll(blocks[s + 1], SIDE, 1)) for s in (0, 2)]
         return jnp.concatenate(pairs, axis=1)
 
-    def lane_of(place):
-        column = place >> 4
-        at = ((column & 3) << 5) + (place & 15) + DEPTH + ((column >> 2) & 1) * SIDE
-        return ((column >> 3) << 7) + (at & 127)
-
-    cells = pick(folded(out_ref, 0, 4 * GROUP), one_hot(lane_of(meta_ref[2:3, 0:CELLS]), 256))
+    cells = pick(folded(out_ref, 0, 4 * GROUP), cell_hot_ref[...])
     newp_ref[...] = cells[0:levels]
     for s in range(species):
         newt_ref[s] = cells[(s + 1) * GROUP : (s + 1) * GROUP + levels]
-    spot = meta_ref[0:1, :]
     turned = jnp.zeros((GROUP, edges), F32)
     for k in range(3):
-        place = spot - k * CELLS
-        at = jnp.where((place >= 0) & (place < CELLS), lane_of(place & (CELLS - 1)), -1)
-        turned = turned + pick(folded(dq_ref, GROUP * k, GROUP), one_hot(at, 256))
+        turned = turned + pick(folded(dq_ref, GROUP * k, GROUP), edge_hot_ref[256 * k : 256 * k + 256])
     sense = meta_ref[1:2, :].astype(F32)
     newv_ref[...] = vel_ref[...] - (grad_scale * sense * flat(invd_ref)) * turned[0:levels]
 
@@ -499,6 +506,18 @@
     )(east, west, south, north)
     from_west = passed_along(to_east, "blk", 1)
     from_east = passed_along(to_west, "blk", -1)
+    core, tcore, cell_hot, edge_hot = pl.pallas_call(
+        settle,
+        out_shape=(
+            shape((rows, 512), F32), shape((trows, 512), F32), shape((CELLS, CELLS), BF16),
+            shape((3 * CELLS, edges), BF16),
+        ),
+        in_specs=[vmem] * 5,
+        out_specs=(vmem,) * 4,
+        compiler_params=pltpu.CompilerParams(vmem_limit_bytes=30 * 2**20),
+        interpret=INTERPRET,
+        name="settle",
+    )(own, trc, south, north, meta)
     block = pltpu.VMEM((levels * 8, 128), F32)
     return pl.pallas_call(
         advance,
@@ -517,7 +536,7 @@
         compiler_params=pltpu.CompilerParams(vmem_limit_bytes=40 * 2**20),
         interpret=INTERPRET,
         name="advance",
-    )(own, trc, south, north, from_west, from_east, meta, velocity, inv_distance)
+    )(core, tcore, from_west, from_east, cell_hot, edge_hot, meta, velocity, inv_distance)
 
 
 def solution(mesh):

time: 77.3 us -> 76.6 us (level)
  waiting for transfers between devices: 7.72 us -> 6.63 us
    ppermute x4, waiting for transfers between devices: 7.72 us -> 6.63 us  [passed_along(): return lax.ppermute(value, axis, pairs)]
    pallas_call x0 -> x1, Pallas kernels: none -> 1.08 us  [per_device(): pl.pallas_call(settle, out_shape=(shape((rows, 512), F32), shape((trows,...]
    pallas_call x1, Pallas kernels: 7.64 us -> 6.78 us  [per_device(): pl.pallas_call(advance, out_shape=(shape((levels, CELLS), F32), shape((le...]
  transfers between devices with their start and end apart: 4 -> 4, of which waited for: 4 -> 4; matrix products, arithmetic and copies ran while one was open for 0% -> 0% of each run, Pallas kernels for 0% -> 1%
where the time goes in v2:
time: 76.6 us; the launch traced here: 75.8 us
  starting transfers between devices  55.5 us (72%)
  Pallas kernels  13 us (17%)
  waiting for transfers between devices  6.63 us (9%)
    ppermute x4, starting transfers between devices, passed_along(): return lax.ppermute(value, axis, pairs)  55.5 us
    pallas_call x1, Pallas kernels, per_device(): pl.pallas_call(advance, out_shape=(shape((levels, CELLS), F32), shape((le...  6.78 us
    ppermute x4, waiting for transfers between devices, passed_along(): return lax.ppermute(value, axis, pairs)  6.63 us
    pallas_call x1, Pallas kernels, per_device(): pl.pallas_call(prepare, out_shape=(shape((rows, CELLS), F32), shape((trow...  4.51 us
  transfers between devices with their start and end apart: 4, of which 4 were waited for; matrix products, arithmetic and copies ran while one was open for 0% of the time, Pallas kernels for 1%

profile of v2, /device:TPU:80, one launch (start us, length us, event | category | flops | bytes accessed | tf_op | source)
XLA Modules:
  0.0 75.8 jit_solution(16469349386904261130)
XLA Ops:
  0.6 0.0 copy-start
  0.6 0.0 copy-start.1
  0.7 4.5 %prepare.1 = (f32[344,256]{1,0:T(8,128)S(1)}, f32[168,256]{1,0:T(8,128)S(1)}, f32[344,128]{1,0:T(8,128)S(1)}, f32[344,128]{1,0:T(8,128)S(1)}, f32[344,128]{1,0:T...) custom-call(s32[6,16]{1,0:T(8,128)} %refs_0_.1, s32[2,768]{1,0:T(2,128)} %refs_1_.1, f32[55,256]{1,0:T(8,128)} %refs_2_.1, ...), custom_call_target="tpu_custom_call" | custom-call | tf_op jit(solution)/shard_map/prepare/pallas_call | solution.py:478
  5.2 6.0 %collective-permute-start = (f32[344,128]{1,0:T(8,128)S(1)}, f32[344,128]{1,0:T(8,128)S(1)}, u32[]{:S(2)}, u32[]{:S(2)}) collective-permute-start(f32[344,128]{1,0:T(8,128)S(1)} %get-tuple-element.18), channel_id=1, source_target_pairs={{0,16},{1,17},{2,18},{3,19},{4,20},{5,21},{6,22},{7,23},{8,24},{9,... | collective-permute-start | bytes 528392 | tf_op jit(solution)/shard_map/ppermute | solution.py:456
  11.2 39.9 %collective-permute-start.1 = (f32[344,128]{1,0:T(8,128)S(1)}, f32[344,128]{1,0:T(8,128)S(1)}, u32[]{:S(2)}, u32[]{:S(2)}) collective-permute-start(f32[344,128]{1,0:T(8,128)S(1)} %get-tuple-element.19), channel_id=1, source_target_pairs={{0,240},{1,241},{2,242},{3,243},{4,244},{5,245},{6,246},{7,247},{8... | collective-permute-start | bytes 528392 | tf_op jit(solution)/shard_map/ppermute | solution.py:456
  51.2 2.6 %collective-permute-done.south_ref = f32[344,128]{1,0:T(8,128)S(1)} collective-permute-done((f32[344,128]{1,0:T(8,128)S(1)}, f32[344,128]{1,0:T(8,128)S(1)}, u32[]{:S(2)}, u32[]{:S(2)}) %collective-permute-start) | collective-permute-done | bytes 176160 | tf_op jit(solution)/shard_map/ppermute | solution.py:456
  53.7 1.2 %collective-permute-done.1.north_ref = f32[344,128]{1,0:T(8,128)S(1)} collective-permute-done((f32[344,128]{1,0:T(8,128)S(1)}, f32[344,128]{1,0:T(8,128)S(1)}, u32[]{:S(2)}, u32[]{:S(2)}) %collective-permute-start.1) | collective-permute-done | bytes 176160 | tf_op jit(solution)/shard_map/ppermute | solution.py:456
  54.9 0.6 pack.1
  55.5 2.0 %collective-permute-start.2 = (f32[176,384]{1,0:T(8,128)S(1)}, f32[176,384]{1,0:T(8,128)S(1)}, u32[]{:S(2)}, u32[]{:S(2)}) collective-permute-start(f32[176,384]{1,0:T(8,128)S(1)} %get-tuple-element.25), channel_id=1, source_target_pairs={{0,1},{1,2},{2,3},{3,4},{4,5},{5,6},{6,7},{7,8},{8,9},{9,10},{10,1... | collective-permute-start | bytes 811016 | tf_op jit(solution)/shard_map/ppermute | solution.py:456
  57.5 7.5 %collective-permute-start.3 = (f32[176,384]{1,0:T(8,128)S(1)}, f32[176,384]{1,0:T(8,128)S(1)}, u32[]{:S(2)}, u32[]{:S(2)}) collective-permute-start(f32[176,384]{1,0:T(8,128)S(1)} %get-tuple-element.26), channel_id=1, source_target_pairs={{0,255},{1,0},{2,1},{3,2},{4,3},{5,4},{6,5},{7,6},{8,7},{9,8},{10,... | collective-permute-start | bytes 811016 | tf_op jit(solution)/shard_map/ppermute | solution.py:456
  65.1 1.1 %settle.1 = (f32[344,512]{1,0:T(8,128)S(1)}, f32[168,512]{1,0:T(8,128)S(1)}, bf16[256,256]{1,0:T(8,128)(2,1)S(1)}, bf16[768,768]{1,0:T(8,128)(2,1)S(1)}) custom-call(f32[344,256]{1,0:T(8,128)S(1)} %get-tuple-element.16.own_ref, f32[168,256]{1,0:T(8,128)S(1)} %get-tuple-element.17.trcl_ref, f32[344,128]{1,0:T(8,128)S(1)} %collective-permute-done.south_ref, ...), custom_call_target="tpu_custom_call" | custom-call | tf_op jit(solution)/shard_map/settle/pallas_call | solution.py:509
  66.2 1.1 %collective-permute-done.2.west_ref = f32[176,384]{1,0:T(8,128)S(1)} collective-permute-done((f32[176,384]{1,0:T(8,128)S(1)}, f32[176,384]{1,0:T(8,128)S(1)}, u32[]{:S(2)}, u32[]{:S(2)}) %collective-permute-start.2) | collective-permute-done | bytes 270368 | tf_op jit(solution)/shard_map/ppermute | solution.py:456
  67.2 1.8 %collective-permute-done.3.east_ref = f32[176,384]{1,0:T(8,128)S(1)} collective-permute-done((f32[176,384]{1,0:T(8,128)S(1)}, f32[176,384]{1,0:T(8,128)S(1)}, u32[]{:S(2)}, u32[]{:S(2)}) %collective-permute-start.3) | collective-permute-done | bytes 270368 | tf_op jit(solution)/shard_map/ppermute | solution.py:456
  69.0 0.0 copy-done
  69.0 0.0 copy-done.1
  69.0 6.8 %advance.1 = (f32[55,256]{1,0:T(8,128)}, f32[55,768]{1,0:T(8,128)}, f32[3,55,256]{2,1,0:T(8,128)}) custom-call(f32[344,512]{1,0:T(8,128)S(1)} %get-tuple-element.21.core_ref, f32[168,512]{1,0:T(8,128)S(1)} %get-tuple-element.22.tcore_ref, f32[176,384]{1,0:T(8,128)S(1)} %collective-permute-done.2.west_ref, f32[176,384]{1,0:T(8,128)S(1)} %collective-permute-done.3.east_ref, ...), custom_call_target="tpu_custom_call" | custom-call | tf_op jit(solution)/shard_map/advance/pallas_call | solution.py:522
Async XLA Ops:
  0.6 68.4 %copy-start = (f32[55,768]{1,0:T(8,128)S(1)}, f32[55,768]{1,0:T(8,128)}, u32[]{:S(2)}) copy-start(f32[55,768]{1,0:T(8,128)} %vel_ref.1) | copy-start | bytes 506884
  0.6 68.4 %copy-start.1 = (f32[768]{0:T(1024)S(1)}, f32[768]{0:T(1024)}, u32[]{:S(2)}) copy-start(f32[768]{0:T(1024)} %invd_ref.1) | copy-start | bytes 9220
  5.2 48.5 %collective-permute-start = (f32[344,128]{1,0:T(8,128)S(1)}, f32[344,128]{1,0:T(8,128)S(1)}, u32[]{:S(2)}, u32[]{:S(2)}) collective-permute-start(f32[344,128]{1,0:T(8,128)S(1)} %get-tuple-element.18), channel_id=1, source_target_pairs={{0,16},{1,17},{2,18},{3,19},{4,20},{5,21},{6,22},{7,23},{8,24},{9,... | collective-permute-start | bytes 528392 | tf_op jit(solution)/shard_map/ppermute | solution.py:456
  11.2 43.7 %collective-permute-start.1 = (f32[344,128]{1,0:T(8,128)S(1)}, f32[344,128]{1,0:T(8,128)S(1)}, u32[]{:S(2)}, u32[]{:S(2)}) collective-permute-start(f32[344,128]{1,0:T(8,128)S(1)} %get-tuple-element.19), channel_id=1, source_target_pairs={{0,240},{1,241},{2,242},{3,243},{4,244},{5,245},{6,246},{7,247},{8... | collective-permute-start | bytes 528392 | tf_op jit(solution)/shard_map/ppermute | solution.py:456
  55.5 11.7 %collective-permute-start.2 = (f32[176,384]{1,0:T(8,128)S(1)}, f32[176,384]{1,0:T(8,128)S(1)}, u32[]{:S(2)}, u32[]{:S(2)}) collective-permute-start(f32[176,384]{1,0:T(8,128)S(1)} %get-tuple-element.25), channel_id=1, source_target_pairs={{0,1},{1,2},{2,3},{3,4},{4,5},{5,6},{6,7},{7,8},{8,9},{9,10},{10,1... | collective-permute-start | bytes 811016 | tf_op jit(solution)/shard_map/ppermute | solution.py:456
  57.5 11.5 %collective-permute-start.3 = (f32[176,384]{1,0:T(8,128)S(1)}, f32[176,384]{1,0:T(8,128)S(1)}, u32[]{:S(2)}, u32[]{:S(2)}) collective-permute-start(f32[176,384]{1,0:T(8,128)S(1)} %get-tuple-element.26), channel_id=1, source_target_pairs={{0,255},{1,0},{2,1},{3,2},{4,3},{5,4},{6,5},{7,6},{8,7},{9,8},{10,... | collective-permute-start | bytes 811016 | tf_op jit(solution)/shard_map/ppermute | solution.py:456

commit v3 on v2

--- a/solution.py
+++ b/solution.py
@@ -61,6 +61,18 @@
     for number, row in enumerate(rows):
         out = jnp.where(at == number, row, out)
     return out
+
+
+def odd_patch():
+    return (lax.axis_index("blk") & 1) == 1
+
+
+def odd_line():
+    return ((lax.axis_index("blk") // SIDE) & 1) == 1
+
+
+def either(flag, x, y):
+    return jnp.where(jnp.broadcast_to(flag, x.shape), x, y)
 
 
 def flat(ref):
@@ -170,6 +182,7 @@
     own_ref[6 * GROUP : 6 * GROUP + 8] = rows8(*lengths, *distances, moved[3 * GROUP : 3 * GROUP + 1])
     column = iota((1, 512), 1)
     part = column >> 7
+    part = either(odd_line(), jnp.where(part < 2, 1 - part, part), part)
     j = column & 127
     sa = sixth(j)
     sb = j - sa * 6
@@ -192,27 +205,32 @@
         ref[rims.shape[0] :] = rest[:, 128 * number : 128 * number + 128]
 
 
-def pack(east_ref, west_ref, south_ref, north_ref, to_east_ref, to_west_ref):
+def pack(east_ref, west_ref, pair_ref, cross_ref, to_pair_ref, to_cross_ref):
     rows = east_ref.shape[0]
-    split = rows - to_east_ref.shape[0]
+    split = rows - to_pair_ref.shape[0]
+    flag = odd_line()
+    south = either(flag, pair_ref[...], cross_ref[...])
+    north = either(flag, cross_ref[...], pair_ref[...])
     cut = DEPTH * DEPTH
     wide = DEPTH * SIDE
     rim = wide + SIDE
-    for part, out, body, corner in (
-        (east_ref, to_east_ref, wide - cut, rim - 1), (west_ref, to_west_ref, 0, wide),
-    ):
+    for out in (to_pair_ref, to_cross_ref):
         out[split:, 0:256] = jnp.zeros((out.shape[0] - split, 256), F32)
-        for begin, end, at in ((0, split, 0), (split, rows, 192)):
-            count = end - begin
-            line = [
-                part[begin:end, 0:rim], south_ref[begin:end, body : body + cut],
-                north_ref[begin:end, body : body + cut], south_ref[begin:end, corner : corner + 1],
-                north_ref[begin:end, corner : corner + 1], jnp.zeros((count, 6), F32),
-            ]
-            out[0:count, at : at + 192] = jnp.concatenate(line, axis=1)
-
-
-def settle(own_ref, trcl_ref, south_ref, north_ref, meta_ref, core_ref, tcore_ref, cell_hot_ref, edge_hot_ref):
+    for begin, end, at in ((0, split, 0), (split, rows, 192)):
+        count = end - begin
+        lines = []
+        for part, body, corner in ((east_ref, wide - cut, rim - 1), (west_ref, 0, wide)):
+            lines.append(jnp.concatenate([
+                part[begin:end, 0:rim], south[begin:end, body : body + cut], north[begin:end, body : body + cut],
+                south[begin:end, corner : corner + 1], north[begin:end, corner : corner + 1],
+                jnp.zeros((count, 6), F32),
+            ], axis=1))
+        flag = odd_patch()
+        to_pair_ref[0:count, at : at + 192] = either(flag, lines[1], lines[0])
+        to_cross_ref[0:count, at : at + 192] = either(flag, lines[0], lines[1])
+
+
+def settle(own_ref, trcl_ref, pair_ref, cross_ref, meta_ref, core_ref, tcore_ref, cell_hot_ref, edge_hot_ref):
     trows = trcl_ref.shape[0]
     q = iota((1, 512), 1)
     qa = q >> 5
@@ -223,7 +241,10 @@
     src = jnp.where(inside, qa * SIDE + qb, -1)
     rsrc = jnp.where(below, qa * DEPTH + qb + DEPTH, jnp.where(above, 128 + qa * DEPTH + qb - SIDE, -1))
     tsrc = jnp.where(qb == -1, 96 + qa, jnp.where(qb == SIDE, 128 + 96 + qa, -1))
-    sn_hi, sn_lo = halves(jnp.concatenate([south_ref[...], north_ref[...]], axis=1))
+    flag = odd_line()
+    south = either(flag, pair_ref[...], cross_ref[...])
+    north = either(flag, cross_ref[...], pair_ref[...])
+    sn_hi, sn_lo = halves(jnp.concatenate([south, north], axis=1))
     own_hot = one_hot(src, 256)
     rim_hot = one_hot(rsrc, 256)
     core_ref[...] = pick(own_ref[...], own_hot) + (dot(sn_hi, rim_hot) + dot(sn_lo, rim_hot))
@@ -244,7 +265,7 @@
 
 
 def advance(
-    core_ref, tcore_ref, west_ref, east_ref, cell_hot_ref, edge_hot_ref, meta_ref, vel_ref, invd_ref,
+    core_ref, tcore_ref, pair_ref, cross_ref, cell_hot_ref, edge_hot_ref, meta_ref, vel_ref, invd_ref,
     newp_ref, newv_ref, newt_ref,
     big_ref, trc_ref, hist_ref, t_ref, f_ref, inv_ref, al_ref, be_ref, out_ref, dq_ref, flow_ref,
 ):
@@ -261,7 +282,10 @@
     inside = (qb >= 0) & (qb < SIDE)
     below = (qb >= -DEPTH) & (qb < 0)
     above = (qb >= SIDE) & (qb < SIDE + DEPTH)
-    for side, ref in ((0, west_ref), (6, east_ref)):
+    flag = odd_patch()
+    west = either(flag, pair_ref[...], cross_ref[...])
+    east = either(flag, cross_ref[...], pair_ref[...])
+    for side, value in ((0, west), (6, east)):
         qa = (q >> 5) - (PAD_A - DEPTH if side == 0 else 0)
         src = jnp.where(
             inside, qa * SIDE + qb,
@@ -273,7 +297,7 @@
             inside, 96 + qb, jnp.where(qb == -1, 184, jnp.where(qb == SIDE, 185, -1))
         )
         tsrc = jnp.where(qa == near, tsrc, -1)
-        hi, lo = halves(ref[...])
+        hi, lo = halves(value)
         hot = one_hot(src, 256)
         thot = one_hot(tsrc, 256)
         late_hot = one_hot(jnp.where(src >= 0, src + 64, -1), 256)
@@ -450,9 +474,12 @@
     newv_ref[...] = vel_ref[...] - (grad_scale * sense * flat(invd_ref)) * turned[0:levels]
 
 
-def passed_along(value, axis, steps):
+def swapped(value, axis, steps, first):
     count = lax.axis_size(axis)
-    pairs = [(source, (source + steps) % count) for source in range(count)]
+    pairs = []
+    for source in range(count):
+        onward = (source // steps) % 2 == first
+        pairs.append((source, (source + (steps if onward else -steps)) % count))
     return lax.ppermute(value, axis, pairs)
 
 
@@ -492,10 +519,10 @@
         interpret=INTERPRET,
         name="prepare",
     )(*inputs)
-    south = passed_along(up, "blk", stride)
-    north = passed_along(down, "blk", -stride)
+    line_pair = swapped(up, "blk", stride, 0)
+    line_cross = swapped(down, "blk", stride, 1)
     half = shape((rows - trows, 384), F32)
-    to_east, to_west = pl.pallas_call(
+    to_pair, to_cross = pl.pallas_call(
         pack,
         out_shape=(half, half),
         in_specs=[vmem] * 4,
@@ -503,9 +530,9 @@
         compiler_params=pltpu.CompilerParams(vmem_limit_bytes=40 * 2**20),
         interpret=INTERPRET,
         name="pack",
-    )(east, west, south, north)
-    from_west = passed_along(to_east, "blk", 1)
-    from_east = passed_along(to_west, "blk", -1)
+    )(east, west, line_pair, line_cross)
+    from_cross = swapped(to_cross, "blk", 1, 1)
+    from_pair = swapped(to_pair, "blk", 1, 0)
     core, tcore, cell_hot, edge_hot = pl.pallas_call(
         settle,
         out_shape=(
@@ -517,7 +544,7 @@
         compiler_params=pltpu.CompilerParams(vmem_limit_bytes=30 * 2**20),
         interpret=INTERPRET,
         name="settle",
-    )(own, trc, south, north, meta)
+    )(own, trc, line_pair, line_cross, meta)
     block = pltpu.VMEM((levels * 8, 128), F32)
     return pl.pallas_call(
         advance,
@@ -536,7 +563,7 @@
         compiler_params=pltpu.CompilerParams(vmem_limit_bytes=40 * 2**20),
         interpret=INTERPRET,
         name="advance",
-    )(core, tcore, from_west, from_east, cell_hot, edge_hot, meta, velocity, inv_distance)
+    )(core, tcore, from_pair, from_cross, cell_hot, edge_hot, meta, velocity, inv_distance)
 
 
 def solution(mesh):

time: 76.6 us -> 77.6 us (1.013)
  waiting for transfers between devices: 6.63 us -> 7.51 us
    ppermute x4, waiting for transfers between devices: 6.63 us -> 7.51 us  [swapped(): return lax.ppermute(value, axis, pairs)]
  transfers between devices with their start and end apart: 4 -> 4, of which waited for: 4 -> 2; matrix products, arithmetic and copies ran while one was open for 0% -> 0% of each run, Pallas kernels for 1% -> 1%
where the time goes in v3:
time: 77.6 us; the launch traced here: 77.4 us
  starting transfers between devices  56.2 us (72%)
  Pallas kernels  13 us (17%)
  waiting for transfers between devices  7.51 us (10%)
    ppermute x4, starting transfers between devices, swapped(): return lax.ppermute(value, axis, pairs)  56.2 us
    ppermute x4, waiting for transfers between devices, swapped(): return lax.ppermute(value, axis, pairs)  7.51 us
    pallas_call x1, Pallas kernels, per_device(): pl.pallas_call(advance, out_shape=(shape((levels, CELLS), F32), shape((le...  6.79 us
    pallas_call x1, Pallas kernels, per_device(): pl.pallas_call(prepare, out_shape=(shape((rows, CELLS), F32), shape((trow...  4.51 us
  transfers between devices with their start and end apart: 4, of which 2 were waited for; matrix products, arithmetic and copies ran while one was open for 0% of the time, Pallas kernels for 1%

profile of v3, /device:TPU:80, one launch (start us, length us, event | category | flops | bytes accessed | tf_op | source)
XLA Modules:
  0.0 77.4 jit_solution(4699257437528197462)
XLA Ops:
  0.6 0.0 copy-start
  0.6 0.0 copy-start.1
  0.7 4.5 %prepare.1 = (f32[344,256]{1,0:T(8,128)S(1)}, f32[168,256]{1,0:T(8,128)S(1)}, f32[344,128]{1,0:T(8,128)S(1)}, f32[344,128]{1,0:T(8,128)S(1)}, f32[344,128]{1,0:T...) custom-call(s32[6,16]{1,0:T(8,128)} %refs_0_.1, s32[2,768]{1,0:T(2,128)} %refs_1_.1, f32[55,256]{1,0:T(8,128)} %refs_2_.1, ...), custom_call_target="tpu_custom_call" | custom-call | tf_op jit(solution)/shard_map/prepare/pallas_call | solution.py:505
  5.2 6.0 %collective-permute-start = (f32[344,128]{1,0:T(8,128)S(1)}, f32[344,128]{1,0:T(8,128)S(1)}, u32[]{:S(2)}, u32[]{:S(2)}) collective-permute-start(f32[344,128]{1,0:T(8,128)S(1)} %get-tuple-element.18), channel_id=1, source_target_pairs={{0,16},{1,17},{2,18},{3,19},{4,20},{5,21},{6,22},{7,23},{8,24},{9,... | collective-permute-start | bytes 528392 | tf_op jit(solution)/shard_map/ppermute | solution.py:483
  11.2 39.9 %collective-permute-start.1 = (f32[344,128]{1,0:T(8,128)S(1)}, f32[344,128]{1,0:T(8,128)S(1)}, u32[]{:S(2)}, u32[]{:S(2)}) collective-permute-start(f32[344,128]{1,0:T(8,128)S(1)} %get-tuple-element.19), channel_id=1, source_target_pairs={{0,240},{1,241},{2,242},{3,243},{4,244},{5,245},{6,246},{7,247},{8... | collective-permute-start | bytes 528392 | tf_op jit(solution)/shard_map/ppermute | solution.py:483
  51.2 0.0 collective-permute-done.pair_ref
  51.2 4.5 %collective-permute-done.1.cross_ref = f32[344,128]{1,0:T(8,128)S(1)} collective-permute-done((f32[344,128]{1,0:T(8,128)S(1)}, f32[344,128]{1,0:T(8,128)S(1)}, u32[]{:S(2)}, u32[]{:S(2)}) %collective-permute-start.1) | collective-permute-done | bytes 176160 | tf_op jit(solution)/shard_map/ppermute | solution.py:483
  55.7 0.6 pack.1
  56.3 2.0 %collective-permute-start.2 = (f32[176,384]{1,0:T(8,128)S(1)}, f32[176,384]{1,0:T(8,128)S(1)}, u32[]{:S(2)}, u32[]{:S(2)}) collective-permute-start(f32[176,384]{1,0:T(8,128)S(1)} %get-tuple-element.25), channel_id=1, source_target_pairs={{0,1},{1,0},{2,3},{3,2},{4,5},{5,4},{6,7},{7,6},{8,9},{9,8},{10,11... | collective-permute-start | bytes 811016 | tf_op jit(solution)/shard_map/ppermute | solution.py:483
  58.2 8.2 %collective-permute-start.3 = (f32[176,384]{1,0:T(8,128)S(1)}, f32[176,384]{1,0:T(8,128)S(1)}, u32[]{:S(2)}, u32[]{:S(2)}) collective-permute-start(f32[176,384]{1,0:T(8,128)S(1)} %get-tuple-element.26), channel_id=1, source_target_pairs={{0,255},{1,2},{2,1},{3,4},{4,3},{5,6},{6,5},{7,8},{8,7},{9,10},{10... | collective-permute-start | bytes 811016 | tf_op jit(solution)/shard_map/ppermute | solution.py:483
  66.5 1.1 %settle.1 = (f32[344,512]{1,0:T(8,128)S(1)}, f32[168,512]{1,0:T(8,128)S(1)}, bf16[256,256]{1,0:T(8,128)(2,1)S(1)}, bf16[768,768]{1,0:T(8,128)(2,1)S(1)}) custom-call(f32[344,256]{1,0:T(8,128)S(1)} %get-tuple-element.16.own_ref, f32[168,256]{1,0:T(8,128)S(1)} %get-tuple-element.17.trcl_ref, f32[344,128]{1,0:T(8,128)S(1)} %collective-permute-done.pair_ref, ...), custom_call_target="tpu_custom_call" | custom-call | tf_op jit(solution)/shard_map/settle/pallas_call | solution.py:536
  67.6 0.0 collective-permute-done.2.pair_ref
  67.6 3.0 %collective-permute-done.3.cross_ref = f32[176,384]{1,0:T(8,128)S(1)} collective-permute-done((f32[176,384]{1,0:T(8,128)S(1)}, f32[176,384]{1,0:T(8,128)S(1)}, u32[]{:S(2)}, u32[]{:S(2)}) %collective-permute-start.3) | collective-permute-done | bytes 270368 | tf_op jit(solution)/shard_map/ppermute | solution.py:483
  70.6 0.0 copy-done
  70.6 0.0 copy-done.1
  70.6 6.8 %advance.1 = (f32[55,256]{1,0:T(8,128)}, f32[55,768]{1,0:T(8,128)}, f32[3,55,256]{2,1,0:T(8,128)}) custom-call(f32[344,512]{1,0:T(8,128)S(1)} %get-tuple-element.21.core_ref, f32[168,512]{1,0:T(8,128)S(1)} %get-tuple-element.22.tcore_ref, f32[176,384]{1,0:T(8,128)S(1)} %collective-permute-done.2.pair_ref, f32[176,384]{1,0:T(8,128)S(1)} %collective-permute-done.3.cross_ref, ...), custom_call_target="tpu_custom_call" | custom-call | tf_op jit(solution)/shard_map/advance/pallas_call | solution.py:549
Async XLA Ops:
  0.6 70.0 %copy-start = (f32[55,768]{1,0:T(8,128)S(1)}, f32[55,768]{1,0:T(8,128)}, u32[]{:S(2)}) copy-start(f32[55,768]{1,0:T(8,128)} %vel_ref.1) | copy-start | bytes 506884
  0.6 70.0 %copy-start.1 = (f32[768]{0:T(1024)S(1)}, f32[768]{0:T(1024)}, u32[]{:S(2)}) copy-start(f32[768]{0:T(1024)} %invd_ref.1) | copy-start | bytes 9220
  5.2 46.0 %collective-permute-start = (f32[344,128]{1,0:T(8,128)S(1)}, f32[344,128]{1,0:T(8,128)S(1)}, u32[]{:S(2)}, u32[]{:S(2)}) collective-permute-start(f32[344,128]{1,0:T(8,128)S(1)} %get-tuple-element.18), channel_id=1, source_target_pairs={{0,16},{1,17},{2,18},{3,19},{4,20},{5,21},{6,22},{7,23},{8,24},{9,... | collective-permute-start | bytes 528392 | tf_op jit(solution)/shard_map/ppermute | solution.py:483
  11.2 44.5 %collective-permute-start.1 = (f32[344,128]{1,0:T(8,128)S(1)}, f32[344,128]{1,0:T(8,128)S(1)}, u32[]{:S(2)}, u32[]{:S(2)}) collective-permute-start(f32[344,128]{1,0:T(8,128)S(1)} %get-tuple-element.19), channel_id=1, source_target_pairs={{0,240},{1,241},{2,242},{3,243},{4,244},{5,245},{6,246},{7,247},{8... | collective-permute-start | bytes 528392 | tf_op jit(solution)/shard_map/ppermute | solution.py:483
  56.3 11.3 %collective-permute-start.2 = (f32[176,384]{1,0:T(8,128)S(1)}, f32[176,384]{1,0:T(8,128)S(1)}, u32[]{:S(2)}, u32[]{:S(2)}) collective-permute-start(f32[176,384]{1,0:T(8,128)S(1)} %get-tuple-element.25), channel_id=1, source_target_pairs={{0,1},{1,0},{2,3},{3,2},{4,5},{5,4},{6,7},{7,6},{8,9},{9,8},{10,11... | collective-permute-start | bytes 811016 | tf_op jit(solution)/shard_map/ppermute | solution.py:483
  58.2 12.4 %collective-permute-start.3 = (f32[176,384]{1,0:T(8,128)S(1)}, f32[176,384]{1,0:T(8,128)S(1)}, u32[]{:S(2)}, u32[]{:S(2)}) collective-permute-start(f32[176,384]{1,0:T(8,128)S(1)} %get-tuple-element.26), channel_id=1, source_target_pairs={{0,255},{1,2},{2,1},{3,4},{4,3},{5,6},{6,5},{7,8},{8,7},{9,10},{10... | collective-permute-start | bytes 811016 | tf_op jit(solution)/shard_map/ppermute | solution.py:483
